TPU v7x, 32 devices: a whole 2x2x4 slice. The times are simulated.
32 devices in a mesh: context: 2 (over core), tensor: 4 (over y, x), fsdp: 4 (over z).
Axes of the slice: x: 2, y: 2, z: 4, core: 2. Of those that a mesh axis runs over, the one named last changes fastest.
Arguments:
- input_raw: bfloat16 [4, 1024, 5120], P('fsdp', ('context', 'tensor')), may hold values from -6 to 6
- state_proj_raw: bfloat16 [4, 1024, 256], P('fsdp', ('context', 'tensor')), may hold values from -6 to 6
- gate_branch: bfloat16 [4, 1024, 5120], P('fsdp', ('context', 'tensor')), may hold values from -6 to 6
- step_raw: bfloat16 [4, 1024, 80], P('fsdp', ('context', 'tensor')), may hold values from -6 to 6
- convolution_taps: float32 [4, 5376], replicated, may hold values from -3 to 3
- convolution_bias: float32 [5376], replicated, may hold values from -3 to 3
- step_bias: float32 [80], P('tensor'), may hold values from -1.5 to 0.5
- decay_log_rate: float32 [80], P('tensor'), may hold values from -13 to -2, as said below
- skip_weight: float32 [80], P('tensor'), may hold values from 0.5 to 2
- gated_norm_gain: float32 [5120], P('tensor'), may hold values from 0.1 to 1.9
- output_weight: bfloat16 [5120, 2560], P('tensor', 'fsdp'), may hold values from -0.078125 to 0.078125
- adapter_down: bfloat16 [5120, 16], P('tensor'), may hold values from -0.078125 to 0.078125
- adapter_up: bfloat16 [16, 2560], replicated, may hold values from -0.29882812 to 0.29882812
- cotangent: bfloat16 [4, 1024, 2560], P('fsdp', ('context', 'tensor')), may hold values from -6 to 6
Outputs:
- mixed: bfloat16 [4, 1024, 2560], P('fsdp', ('context', 'tensor'))
- grad_a: float32 [5120, 16], P('tensor')
- grad_b: float32 [16, 2560], replicated
Inputs may be any that keep to these rules, and one draw needn't show every extreme that they name: `decay_log_rate`: logarithms of positive decay rates.
All inputs are finite; a program needn't handle non-finite values.
Results may differ from a plain program's by a relative error of at most 0.017.
Values may be sent and summed in bfloat16 or wider, within the bound.
A program may use at most 128 MiB of HBM per device.

v0:
```python
import functools
import math

import jax
import jax.numpy as jnp
from jax import lax
from jax.experimental import pallas as pl
from jax.experimental.pallas import tpu as pltpu
from jax.sharding import PartitionSpec as P

EPS = 1e-05
MESH = pl.DeviceIdType.MESH
HI = lax.Precision.HIGHEST
BF = jnp.bfloat16
F32 = jnp.float32


def dot(a, b, ca=1, cb=0, precision=None):
    return lax.dot_general(
        a, b, (((ca,), (cb,)), ((), ())), preferred_element_type=F32, precision=precision
    )


def iota(shape, dim):
    return lax.broadcasted_iota(jnp.int32, shape, dim)


def kernel(
    nt, nf, nc, hl,
    x_ref, bc_ref, z_ref, dt_ref, taps_ref, bias_ref, sb_ref, dr_ref, sk_ref, gain_ref, w_ref, down_ref, up_ref, cot_ref,
    mixed_ref, ga_ref, gb_ref,
    halo_x, halo_bc, x_send, x_all, z_all, bc_all, dt_all, wbuf, a_s, step_s, at_s, stept_s,
    stl, msg, st_in, inc_s, e_s, y_s, g_s, adx, ad_in, ag_own, ag_all, gb_own, gb_in, comb, comb_c, comb2, comb_f,
    fin, rs_send, rs_recv,
    h_ss, h_rs, dt_ss, dt_rs, bc_ss, bc_rs, x_ss, x_rs, z_ss, z_rs, w_ss, w_rs, wf_ss, wf_rs, st_ss, st_rs,
    ad_ss, ad_rs, ag_ss, ag_rs, ga_ss, ga_rs, cc_ss, cc_rs, cf_ss, cf_rs, fin_ss, fin_rs, r_ss, r_rs, loc,
):
    t = lax.axis_index("tensor")
    f = lax.axis_index("fsdp")
    c = lax.axis_index("context")
    L = x_ref.shape[0]
    LW = x_all.shape[1]
    W = w_ref.shape[1]
    N = bc_ref.shape[1] // 2
    R = w_ref.shape[0] // nc
    HS = LW // hl
    idx = c * nt + t
    total = nc * nt

    def tp(e):
        return lax.rem(t + e, nt)

    def place(i):
        return {"context": i // nt, "tensor": lax.rem(i, nt)}

    def copy(src, dst, ss, rs, dev):
        cp = pltpu.make_async_remote_copy(
            src_ref=src, dst_ref=dst, send_sem=ss, recv_sem=rs, device_id=dev, device_id_type=MESH
        )
        cp.start()
        return cp

    nxt, prv = lax.rem(idx + 1, total), lax.rem(idx + total - 1, total)
    bar = pltpu.get_barrier_semaphore()
    greet = [{"tensor": tp(e)} for e in range(1, nt)]
    greet += [{"fsdp": lax.rem(f + d, nf)} for d in range(1, nf)]
    greet += [{"context": lax.rem(c + k, nc)} for k in range(1, nc)]
    greet += [place(nxt), place(prv)]
    for dev in greet:
        pl.semaphore_signal(bar, inc=1, device_id=dev, device_id_type=MESH)
    pl.semaphore_wait(bar, len(greet))
    sent = []

    h1 = copy(x_ref.at[L - 16 : L, :], halo_x, h_ss.at[0], h_rs.at[0], place(nxt))
    h2 = copy(bc_ref.at[L - 16 : L, :], halo_bc, h_ss.at[1], h_rs.at[1], place(nxt))
    own_rows = pl.ds(pl.multiple_of(t * L, L), L)
    dts = [copy(dt_ref, dt_all.at[t], dt_ss.at[e], dt_rs.at[e], {"tensor": tp(e)}) for e in range(1, nt)]
    share = pl.ds(pl.multiple_of(c * R, 16), R)
    ws = [
        copy(w_ref.at[share, :], wbuf.at[d, share, :], w_ss.at[d], w_rs.at[d], {"fsdp": lax.rem(f + d, nf)})
        for d in range(1, nf)
    ]
    own_w = pltpu.make_async_copy(w_ref, wbuf.at[0], loc.at[0])
    own_w.start()
    own_cols = pl.ds(pl.multiple_of(t * LW, 128), LW)
    own_z = pltpu.make_async_copy(z_ref.at[:, own_cols], z_all.at[own_rows, :], loc.at[1])
    own_z.start()
    dt_all[t] = dt_ref[...]

    def send_gate(e):
        cols = pl.ds(pl.multiple_of(tp(e) * LW, 128), LW)
        return copy(z_ref.at[:, cols], z_all.at[own_rows, :], z_ss.at[e], z_rs.at[e], {"tensor": tp(e)})

    zs = [send_gate(1)]
    h1.wait()
    h2.wait()
    live = (idx > 0).astype(F32)

    def conv(src, halo, col, tap_col):
        lanes = pl.ds(col, 128)
        wide = pl.ds(tap_col, 128)
        ext = jnp.concatenate([halo[8:16, lanes].astype(F32) * live, src[:, lanes].astype(F32)], axis=0)
        acc = bias_ref[:, wide] + taps_ref[0:1, wide] * ext[5 : 5 + L]
        for k in range(1, 4):
            acc = acc + taps_ref[k : k + 1, wide] * ext[5 + k : 5 + k + L]
        return (acc / (1.0 + jnp.exp(-acc))).astype(BF)

    wide0 = x_ref.shape[1]
    for j in range(2 * N // 128):
        bc_all[own_rows, j * 128 : (j + 1) * 128] = conv(bc_ref, halo_bc, j * 128, wide0 + j * 128)
    bcs = [
        copy(bc_all.at[own_rows, :], bc_all.at[own_rows, :], bc_ss.at[e], bc_rs.at[e], {"tensor": tp(e)})
        for e in range(1, nt)
    ]
    xs = []

    def conv_group(e, store):
        base = tp(e) * LW

        def lap(j, carry):
            col = pl.multiple_of(base + j * 128, 128)
            store(pl.ds(pl.multiple_of(j * 128, 128), 128), conv(x_ref, halo_x, col, col))
            return carry

        lax.fori_loop(0, LW // 128, lap, 0)

    for e in range(1, nt):
        def put(lanes, val, e=e):
            x_send[e - 1, :, lanes] = val

        conv_group(e, put)
        xs.append(copy(x_send.at[e - 1], x_all.at[own_rows, :], x_ss.at[e], x_rs.at[e], {"tensor": tp(e)}))
    for e in range(2, nt):
        zs.append(send_gate(e))

    def put_own(lanes, val):
        x_all[own_rows, lanes] = val

    conv_group(0, put_own)
    e_s[...] = (iota((128, LW), 1) // HS == iota((128, LW), 0)).astype(F32)
    spread16 = e_s[...].astype(BF)

    def spread(rows):
        return dot(jnp.broadcast_to(rows, (8, 128)), e_s[...], precision=HI)

    for cp in dts:
        cp.wait()
    HR = at_s.shape[1]
    HA = dt_ref.shape[0]
    sel = ((iota((HA, 128), 0) == iota((HA, 128), 1) + t * hl) & (iota((HA, 128), 1) < hl)).astype(BF)
    sel_t = ((iota((HR, HA), 1) == iota((HR, HA), 0) + t * hl) & (iota((HR, HA), 0) < hl)).astype(BF)
    eye = (iota((HR, 128), 0) == iota((HR, 128), 1)).astype(F32)
    place_head = (iota((hl, 128), 0) == iota((hl, 128), 1)).astype(F32)
    hp = [
        dot(jnp.broadcast_to(v[...], (8, hl)), place_head, precision=HI)[0:1, :] for v in (sb_ref, dr_ref, sk_ref)
    ]
    hp_t = [dot(eye, jnp.broadcast_to(v, (8, 128)), 1, 1, HI)[:, 0:1] for v in hp[0:2]]
    tri = (iota((L, L), 0) >= iota((L, L), 1)).astype(F32)

    def softplus(v):
        return jnp.maximum(v, 0.0) + jnp.log1p(jnp.exp(-jnp.abs(v)))

    for b in range(nt):
        rows = slice(b * L, (b + 1) * L)
        raw = dt_all[b]
        step = softplus(dot(raw, sel, 0, 0) + hp[0])
        step_s[rows, :] = step
        a_s[rows, :] = dot(tri, -step * jnp.exp(hp[1]), precision=HI)
        step_t = softplus(dot(sel_t, raw) + hp_t[0])
        stept_s[b] = step_t
        at_s[b] = dot(-step_t * jnp.exp(hp_t[1]), tri, 1, 1, HI)
    for cp in bcs:
        cp.wait()
    for cp in xs:
        cp.wait()

    state = jnp.zeros((N, LW), F32)
    before = jnp.zeros((1, 128), F32)
    for b in range(nt):
        rows = slice(b * L, (b + 1) * L)
        stl[b, 0:N, :] = state
        stl[b, N : N + 8, :] = spread(jnp.exp(before))
        a = a_s[rows, :]
        last = a[L - 1 : L, :]
        weight = (jnp.exp(last - a) * step_s[rows, :]).astype(BF)
        xw = (x_all[rows, :].astype(F32) * dot(weight, spread16)).astype(BF)
        state = spread(jnp.exp(last))[0:1, :] * state + dot(bc_all[rows, 0:N], xw, 0, 0)
        before = before + last
    msg[0:N, :] = state
    msg[N : N + 8, :] = spread(before)
    sts = [
        copy(msg, st_in.at[c], st_ss.at[k], st_rs.at[k], {"context": lax.rem(c + k, nc)})
        for k in range(1, nc)
    ]

    left = iota((L, 2 * HS), 1) < HS

    def inner(b, carry):
        rows = pl.ds(pl.multiple_of(b * L, L), L)
        gram = dot(bc_all[rows, N : 2 * N], bc_all[rows, 0:N], 1, 1)
        gram = jnp.where(iota((L, L), 0) >= iota((L, L), 1), gram, 0.0)
        a = a_s[rows, :]
        at = at_s[b]
        stt = stept_s[b]
        for pair in range(hl // 2):
            lanes = slice(pair * 2 * HS, (pair + 1) * 2 * HS)
            xp = x_all[rows, lanes]
            out = []
            for h in (2 * pair, 2 * pair + 1):
                gap = jnp.minimum(a[:, h : h + 1] - at[h : h + 1, :], 0.0)
                m = (jnp.exp(gap) * gram * stt[h : h + 1, :]).astype(BF)
                out.append(dot(m, xp))
            y_s[rows, lanes] = jnp.where(left, out[0], out[1])
        return carry

    lax.fori_loop(0, nt, inner, 0)

    for cp in sts:
        cp.wait()
    inc_s[...] = jnp.zeros_like(inc_s)

    def chain(k, carry):
        inc_s[...] = jnp.exp(st_in[k, N : N + 1, :]) * inc_s[...] + st_in[k, 0:N, :]
        return carry

    lax.fori_loop(0, c, chain, 0)
    for cp in zs:
        cp.wait()
    own_z.wait()
    skip = spread(hp[2])[0:1, :]
    ones = jnp.ones((8, LW), BF)

    def gate(b, carry):
        rows = pl.ds(pl.multiple_of(b * L, L), L)
        start = (stl[b, 0:N, :] + stl[b, N : N + 1, :] * inc_s[...]).astype(BF)
        reach = dot(jnp.exp(a_s[rows, :]).astype(BF), spread16)
        y = y_s[rows, :] + reach * dot(bc_all[rows, N : 2 * N], start)
        y = y + skip * x_all[rows, :].astype(F32)
        z = z_all[rows, :].astype(F32)
        g = y * (z / (1.0 + jnp.exp(-z)))
        out = (g * gain_ref[...]).astype(BF)
        g_s[rows, :] = out
        adx[b, 0:16, :] = dot(down_ref[...], out, 1, 1)
        adx[b, 16:24, :] = dot(ones, (g * g).astype(BF), 1, 1)
        return carry

    lax.fori_loop(0, nt, gate, 0)
    ads = [copy(adx.at[tp(e)], ad_in.at[e], ad_ss.at[e], ad_rs.at[e], {"tensor": tp(e)}) for e in range(1, nt)]

    half = (nt * L) // 2

    def project(d):
        def lap(i, carry):
            rows = pl.ds(pl.multiple_of(i * half, half), half)
            rs_send[d, rows, :] = dot(g_s[rows, :], wbuf[d]).astype(BF)
            return carry

        lax.fori_loop(0, 2, lap, 0)

    def scatter(d):
        return [
            copy(
                rs_send.at[d, pl.ds(pl.multiple_of(tp(e) * L, L), L), :],
                rs_recv.at[d, e - 1], r_ss.at[d, e], r_rs.at[d, e], {"tensor": tp(e)},
            )
            for e in range(1, nt)
        ]

    own_w.wait()
    project(0)
    for cp in ads:
        cp.wait()
    red = adx[t]
    for e in range(1, nt):
        red = red + ad_in[e]
    scale_row = lax.rsqrt(red[16:17, :] / (LW * nt) + EPS)
    ad16 = red[0:16, :].astype(BF)
    factor = 2.0 / math.sqrt(L * nt * nc * nf)
    cot = cot_ref[...]
    ag_own[...] = factor * scale_row * dot(up_ref[...], cot, 1, 1)
    ags = [copy(ag_own, ag_all.at[t], ag_ss.at[e], ag_rs.at[e], {"tensor": tp(e)}) for e in range(1, nt)]
    gb_own[...] = dot((factor * scale_row * ad16.astype(F32)).astype(BF), cot)
    part = gb_own.shape[1] // nt
    own_part = pl.ds(pl.multiple_of(t * part, 128), part)
    gbs = [
        copy(
            gb_own.at[:, pl.ds(pl.multiple_of(tp(e) * part, 128), part)],
            gb_in.at[e], ga_ss.at[e], ga_rs.at[e], {"tensor": tp(e)},
        )
        for e in range(1, nt)
    ]
    sent += scatter(0)
    for cp in ags + gbs:
        cp.wait()
    ag_all[t] = ag_own[...]
    grad = jnp.zeros((16, LW), F32)
    for s in range(nt):
        grad = grad + dot(ag_all[s].astype(BF), g_s[s * L : (s + 1) * L, :])
    comb[:, 0:LW] = grad
    acc = gb_own[:, own_part]
    for e in range(1, nt):
        acc = acc + gb_in[e]
    comb[:, LW : LW + part] = acc
    ccs = [copy(comb, comb_c.at[k], cc_ss.at[k], cc_rs.at[k], {"context": lax.rem(c + k, nc)}) for k in range(1, nc)]
    wfs = []
    for d in range(1, nf):
        ws[d - 1].wait()
        wfs.append([
            copy(wbuf.at[d, share, :], wbuf.at[d, share, :], wf_ss.at[d, k], wf_rs.at[d, k], {"context": lax.rem(c + k, nc)})
            for k in range(1, nc)
        ])
    for cp in ccs:
        cp.wait()
    acc = comb[...]
    for k in range(1, nc):
        acc = acc + comb_c[k]
    comb2[...] = acc
    cfs = [copy(comb2, comb_f.at[k], cf_ss.at[k], cf_rs.at[k], {"fsdp": lax.rem(f + k, nf)}) for k in range(1, nf)]
    for d in range(1, nf):
        for cp in wfs[d - 1]:
            cp.wait()
        project(d)
        sent += scatter(d)
    for cp in cfs:
        cp.wait()
    acc = comb2[...]
    for k in range(1, nf):
        acc = acc + comb_f[k]
    ga_ref[...] = acc[:, 0:LW]
    fin[t] = acc[:, LW:]
    fins = [copy(fin.at[t], fin.at[t], fin_ss.at[e], fin_rs.at[e], {"tensor": tp(e)}) for e in range(1, nt)]
    scale_col = dot(jnp.broadcast_to(scale_row, (8, L)), jnp.full((8, 128), 0.125, F32), 0, 0, HI)[:, 0:1]
    for d in range(nf):
        for cp in sent[d * (nt - 1) : (d + 1) * (nt - 1)]:
            cp.wait()
        cols = pl.ds(pl.multiple_of(lax.rem(f + nf - d, nf) * W, 128), W)
        acc = rs_send[d, own_rows, :].astype(F32)
        for e in range(1, nt):
            acc = acc + rs_recv[d, e - 1].astype(F32)
        acc = acc + 2.0 * dot(ad16, up_ref[:, cols], 0, 0)
        mixed_ref[:, cols] = (scale_col * acc).astype(BF)
    for cp in fins:
        cp.wait()
    for s in range(nt):
        gb_ref[:, s * part : (s + 1) * part] = fin[s]


def shards(x, bc, z, dt, taps, bias, step_bias, rate, skip, gain, w, down, up, cot):
    nt, nf, nc = lax.axis_size("tensor"), lax.axis_size("fsdp"), lax.axis_size("context")
    L, full = x.shape[1], x.shape[2]
    LW, hl, W, M = gain.shape[0], step_bias.shape[0], w.shape[1], cot.shape[2]
    BC = bc.shape[2]
    N = BC // 2
    HR = -(-hl // 8) * 8
    T = nt * L
    part = M // nt
    dt = dt[0].T
    vm = pl.BlockSpec(memory_space=pltpu.VMEM)
    hbm = pl.BlockSpec(memory_space=pl.ANY)
    V = pltpu.VMEM
    D = pltpu.SemaphoreType.DMA
    scratch = [
        V((16, full), BF), V((16, BC), BF), V((nt - 1, L, LW), BF), V((T, LW), BF), V((T, LW), BF),
        V((T, BC), BF), V((nt,) + dt.shape, BF), V((nf, LW, W), BF), V((T, 128), F32), V((T, 128), F32),
        V((nt, HR, L), F32), V((nt, HR, L), F32),
        V((nt, N + 8, LW), F32), V((N + 8, LW), F32), V((nc, N + 8, LW), F32), V((N, LW), F32),
        V((128, LW), F32), V((T, LW), F32), V((T, LW), BF), V((nt, 24, L), F32), V((nt, 24, L), F32),
        V((16, L), F32), V((nt, 16, L), F32), V((16, M), F32), V((nt, 16, part), F32),
        V((16, LW + part), F32), V((nc, 16, LW + part), F32), V((16, LW + part), F32), V((nf, 16, LW + part), F32),
        V((nt, 16, part), F32), V((nf, T, W), BF), V((nf, nt - 1, L, W), BF),
        D((2,)), D((2,)), D((nt,)), D((nt,)), D((nt,)), D((nt,)), D((nt,)), D((nt,)), D((nt,)), D((nt,)),
        D((nf,)), D((nf,)), D((nf, nc)), D((nf, nc)), D((nc,)), D((nc,)),
        D((nt,)), D((nt,)), D((nt,)), D((nt,)), D((nt,)), D((nt,)), D((nc,)), D((nc,)), D((nf,)), D((nf,)),
        D((nt,)), D((nt,)), D((nf, nt)), D((nf, nt)), D((2,)),
    ]
    mixed, ga, gb = pl.pallas_call(
        functools.partial(kernel, nt, nf, nc, hl),
        out_shape=(
            jax.ShapeDtypeStruct((L, M), BF),
            jax.ShapeDtypeStruct((16, LW), F32),
            jax.ShapeDtypeStruct((16, M), F32),
        ),
        in_specs=[vm, vm, hbm, vm, vm, vm, vm, vm, vm, vm, hbm, vm, vm, vm],
        out_specs=(vm, vm, vm),
        scratch_shapes=scratch,
        compiler_params=pltpu.CompilerParams(
            collective_id=0, has_side_effects=True, vmem_limit_bytes=62 * 1024 * 1024
        ),
    )(x[0], bc[0], z[0], dt, taps, bias[None], step_bias[None], rate[None], skip[None], gain[None], w, down.T, up, cot[0])
    return mixed[None], ga.T, gb


def solution(mesh):
    tokens = P("fsdp", ("context", "tensor"), None)
    placed = (
        tokens, tokens, tokens, tokens, P(), P(), P("tensor"), P("tensor"), P("tensor"), P("tensor"),
        P("tensor", "fsdp"), P("tensor", None), P(), tokens,
    )
    return jax.shard_map(
        shards, mesh=mesh, in_specs=placed, out_specs=(tokens, P("tensor", None), P()), check_vma=False
    )
```

profile of v0, /device:TPU:24, one launch (start us, length us, event | category | flops | bytes accessed | tf_op | source)
XLA Modules:
  0.0 115.7 jit_solution(4425383433896568508)
XLA Ops:
  0.6 1.3 %broadcast_in_dim.22.gain_ref = f32[1,1280]{1,0:T(1,128)} reshape(f32[1280]{0:T(1024)} %param.23) | data formatting | bytes 10240 | tf_op jit(solution)/shard_map/broadcast_in_dim | solution.py:389
  1.9 1.4 %broadcast_in_dim.18.bias_ref = f32[1,5376]{1,0:T(1,128)} reshape(f32[5376]{0:T(1024)} %param.19) | data formatting | bytes 43008 | tf_op jit(solution)/shard_map/broadcast_in_dim | solution.py:389
  3.3 109.1 %shard_map.157 = (bf16[128,2560]{1,0:T(8,128)(2,1)}, f32[16,1280]{1,0:T(8,128)}, f32[16,2560]{1,0:T(8,128)}) custom-call(bf16[128,5120]{1,0:T(8,128)(2,1)} %bitcast.13, bf16[128,256]{1,0:T(8,128)(2,1)} %bitcast.18, bf16[128,5120]{1,0:T(8,128)(2,1)} %bitcast.14, bf16[80,128]{1,0:T(8,128)(2,1)} %bitcast.20, f32[4,5376]{1,0:T(4,128)} %taps_ref.1, ...), custom_call_target="tpu_custom_call" | custom-call | tf_op jit(solution)/shard_map/pallas_call | solution.py:376
  112.4 0.0 copy-start.1
  112.4 0.0 copy-start
  112.4 2.0 %copy.20 = bf16[1,128,2560]{2,1,0:T(8,128)(2,1)} copy(bf16[1,128,2560]{2,1,0:T(8,128)(2,1)} %bitcast.15) | data formatting | bytes 1310720
  114.4 0.0 copy-done.1
  114.4 0.6 copy.21
  115.0 0.0 copy-done
  115.0 0.7 copy.22
Async XLA Ops:
  112.4 2.0 %copy-start.1 = (f32[16,1280]{1,0:T(8,128)S(1)}, f32[16,1280]{1,0:T(8,128)}, u32[]{:S(2)}) copy-start(f32[16,1280]{1,0:T(8,128)} %get-tuple-element.7) | copy-start | bytes 245764
  112.4 2.7 %copy-start = (f32[16,2560]{1,0:T(8,128)S(1)}, f32[16,2560]{1,0:T(8,128)}, u32[]{:S(2)}) copy-start(f32[16,2560]{1,0:T(8,128)} %get-tuple-element.14) | copy-start | bytes 491524
where the time goes:
time: 116 us
  Pallas kernels  109 us (94%)
  local copies, waits for them, and re-layouts  5.97 us (5%)
    pallas_call x1, Pallas kernels, shards(): pl.pallas_call(functools.partial(kernel, nt, nf, nc, hl), out_shape=(jax....  109 us
    unnamed x7, local copies, waits for them, and re-layouts  3.32 us

commit v1 on v0

v1 whole, which is shorter than its diff:
```python
import functools
import math

import jax
import jax.numpy as jnp
from jax import lax
from jax.experimental import pallas as pl
from jax.experimental.pallas import tpu as pltpu
from jax.sharding import PartitionSpec as P

EPS = 1e-05
MESH = pl.DeviceIdType.MESH
HI = lax.Precision.HIGHEST
BF = jnp.bfloat16
F32 = jnp.float32
HALO = 16


def dot(a, b, ca=1, cb=0, precision=None):
    return lax.dot_general(
        a, b, (((ca,), (cb,)), ((), ())), preferred_element_type=F32, precision=precision
    )


def iota(shape, dim):
    return lax.broadcasted_iota(jnp.int32, shape, dim)


def pick(values, i):
    out = jnp.int32(values[0])
    for k in range(1, len(values)):
        out = jnp.where(i == k, jnp.int32(values[k]), out)
    return out


def column_chunks(width):
    lanes = width // 128
    first = -(-lanes // 2)
    return [(0, first * 128), (first * 128, (lanes - first) * 128)] if lanes > 1 else [(0, width)]


def kernel(
    nt, nf, nc, hl,
    x_hbm, bc_hbm, z_ref, dt_hbm, taps_hbm, bias_hbm, sb_ref, dr_ref, sk_ref, gain_hbm, w_ref, down_hbm, up_hbm, cot_hbm,
    mixed_ref, ga_ref, gb_ref,
    x_ref, bc_ref, dt_ref, taps_ref, bias_ref, gain_ref, down_ref, up_ref, cot_ref,
    halo_x, halo_bc, x_send, x_all, z_all, bc_all, dt_all, wbuf, a_s, step_s, at_s, stept_s,
    stl, msg, st_in, inc_s, e_s, y_s, g_s, adx, ad_in, ag_own, ag_all, gb_own, gb_in,
    comb, comb_c, comb2, comb_f, seg_own, seg_in, full, fin, rs_send, rs_recv,
    ld, h_ss, h_rs, dt_ss, dt_rs, bc_ss, bc_rs, x_ss, x_rs, z_ss, z_rs, w_ss, w_rs, wf_ss, wf_rs, st_ss, st_rs,
    ad_ss, ad_rs, ag_ss, ag_rs, ga_ss, ga_rs, cc_ss, cc_rs, cf_ss, cf_rs, sg_ss, sg_rs, fin_ss, fin_rs, r_ss, r_rs, loc,
):
    t = lax.axis_index("tensor")
    f = lax.axis_index("fsdp")
    c = lax.axis_index("context")
    L = x_ref.shape[0]
    LW = x_all.shape[1]
    W = w_ref.shape[1]
    N = bc_ref.shape[1] // 2
    R = w_ref.shape[0] // nc
    HS = LW // hl
    idx = c * nt + t
    total = nc * nt
    bits = [1 << i for i in range(nt.bit_length() - 1)]
    chunks = column_chunks(W)
    steps = nf - 1

    def peer(e):
        out = 0
        for bit in bits:
            out = out + bit * lax.rem(lax.div(t, bit) + lax.div(e, bit), 2)
        return out

    def peers():
        return [peer(jnp.int32(e)) for e in range(nt)]

    pt = peers()

    def place(i):
        return {"context": i // nt, "tensor": lax.rem(i, nt)}

    def remote(src, dst, ss, rs, dev):
        return pltpu.make_async_remote_copy(
            src_ref=src, dst_ref=dst, send_sem=ss, recv_sem=rs, device_id=dev, device_id_type=MESH
        )

    def copy(src, dst, ss, rs, dev):
        cp = remote(src, dst, ss, rs, dev)
        cp.start()
        return cp

    loads = []
    for i, (src, dst) in enumerate((
        (x_hbm, x_ref), (bc_hbm, bc_ref), (dt_hbm, dt_ref), (taps_hbm, taps_ref), (bias_hbm, bias_ref),
        (gain_hbm, gain_ref), (down_hbm, down_ref), (up_hbm, up_ref), (cot_hbm, cot_ref),
    )):
        cp = pltpu.make_async_copy(src, dst, ld.at[i])
        cp.start()
        loads.append(cp)
    own_w = pltpu.make_async_copy(w_ref, wbuf.at[f], loc.at[0])
    own_w.start()
    own_rows = pl.ds(pl.multiple_of(t * L, L), L)
    own_cols = pl.ds(pl.multiple_of(t * LW, 128), LW)
    own_z = pltpu.make_async_copy(z_ref.at[:, own_cols], z_all.at[own_rows, :], loc.at[1])
    own_z.start()

    nxt, prv = lax.rem(idx + 1, total), lax.rem(idx + total - 1, total)
    bar = pltpu.get_barrier_semaphore()
    greet = [{"tensor": pt[e]} for e in range(1, nt)]
    greet += [{"fsdp": lax.rem(f + d, nf)} for d in range(1, nf)]
    greet += [{"context": lax.rem(c + k, nc)} for k in range(1, nc)]
    greet += [place(nxt), place(prv)]
    for dev in greet:
        pl.semaphore_signal(bar, inc=1, device_id=dev, device_id_type=MESH)
    for cp in loads:
        cp.wait()
    dt_all[t] = dt_ref[...]
    pl.semaphore_wait(bar, len(greet))

    h1 = copy(x_ref.at[L - HALO : L, :], halo_x, h_ss.at[0], h_rs.at[0], place(nxt))
    h2 = copy(bc_ref.at[L - HALO : L, :], halo_bc, h_ss.at[1], h_rs.at[1], place(nxt))
    dts = [copy(dt_ref, dt_all.at[t], dt_ss.at[e], dt_rs.at[e], {"tensor": pt[e]}) for e in range(1, nt)]
    share = pl.ds(pl.multiple_of(c * R, 16), R)

    def w_copy(dr, s, ch, q):
        cols = pl.ds(chunks[ch][0], chunks[ch][1])
        src = w_ref.at[share, cols] if s == 0 else wbuf.at[q, share, cols]
        to = f + 1 if dr == 0 else f - 1
        return remote(src, wbuf.at[q, share, cols], w_ss.at[dr, s, ch], w_rs.at[dr, s, ch], {"fsdp": to})

    def w_share(dr, s, ch, q, k):
        region = wbuf.at[q, share, pl.ds(chunks[ch][0], chunks[ch][1])]
        return remote(region, region, wf_ss.at[dr, s, ch, k], wf_rs.at[dr, s, ch, k], {"context": lax.rem(c + k, nc)})

    def has_next(dr):
        return f + 1 < nf if dr == 0 else f >= 1

    def sends(dr, s):
        return (f - s >= 0) & (f + 1 < nf) if dr == 0 else (f + s < nf) & (f >= 1)

    def gets(dr, s):
        return f - 1 - s >= 0 if dr == 0 else f + 1 + s < nf

    def came(dr, s):
        return f - 1 - s if dr == 0 else f + 1 + s

    for ch in range(len(chunks)):
        for dr in range(2):
            @pl.when(sends(dr, 0))
            def _(dr=dr, ch=ch):
                w_copy(dr, 0, ch, f).start()

    def w_arrive(s, ch):
        for dr in range(2):
            @pl.when(gets(dr, s))
            def _(dr=dr):
                q = came(dr, s)
                w_copy(dr, s, ch, q).wait_recv()
                if s + 1 < steps:
                    @pl.when(has_next(dr))
                    def _():
                        w_copy(dr, s + 1, ch, q).start()
                for k in range(1, nc):
                    w_share(dr, s, ch, q, k).start()

    table = [sorted(range(nf), key=lambda q, g=g: (abs(q - g), q)) for g in range(nf)]
    order = [pick([table[g][i] for g in range(nf)], f) for i in range(nf)]
    way = [pick([int(table[g][i] > g) for g in range(nf)], f) for i in range(nf)]
    dist = [pick([max(abs(table[g][i] - g) - 1, 0) for g in range(nf)], f) for i in range(nf)]

    def w_ready(slot, ch):
        region = wbuf.at[order[slot], share, pl.ds(chunks[ch][0], chunks[ch][1])]
        for k in range(1, nc):
            remote(
                region, region, wf_ss.at[way[slot], dist[slot], ch, k], wf_rs.at[way[slot], dist[slot], ch, k],
                {"context": lax.rem(c + k, nc)},
            ).wait_recv()

    def send_gate(e):
        cols = pl.ds(pl.multiple_of(pt[e] * LW, 128), LW)
        return copy(z_ref.at[:, cols], z_all.at[own_rows, :], z_ss.at[e], z_rs.at[e], {"tensor": pt[e]})

    early = nt - 1 if nt > 2 else nt
    zs = [send_gate(e) for e in range(1, early)]
    h1.wait()
    h2.wait()
    live = (idx > 0).astype(F32)

    def conv(src, halo, col, tap_col):
        lanes = pl.ds(col, 128)
        wide = pl.ds(tap_col, 128)
        ext = jnp.concatenate([halo[HALO - 8 : HALO, lanes].astype(F32) * live, src[:, lanes].astype(F32)], axis=0)
        acc = bias_ref[:, wide] + taps_ref[0:1, wide] * ext[5 : 5 + L]
        for k in range(1, 4):
            acc = acc + taps_ref[k : k + 1, wide] * ext[5 + k : 5 + k + L]
        return (acc / (1.0 + jnp.exp(-acc))).astype(BF)

    wide0 = x_ref.shape[1]
    for j in range(2 * N // 128):
        bc_all[own_rows, j * 128 : (j + 1) * 128] = conv(bc_ref, halo_bc, j * 128, wide0 + j * 128)
    bcs = [
        copy(bc_all.at[own_rows, :], bc_all.at[own_rows, :], bc_ss.at[e], bc_rs.at[e], {"tensor": pt[e]})
        for e in range(1, nt)
    ]
    xs = []

    def conv_group(e, store):
        base = pt[e] * LW

        def lap(j, carry):
            col = pl.multiple_of(base + j * 128, 128)
            store(pl.ds(pl.multiple_of(j * 128, 128), 128), conv(x_ref, halo_x, col, col))
            return carry

        lax.fori_loop(0, LW // 128, lap, 0)

    for e in range(nt - 1, 0, -1):
        def put(lanes, val, e=e):
            x_send[e - 1, :, lanes] = val

        conv_group(e, put)
        xs.append(copy(x_send.at[e - 1], x_all.at[own_rows, :], x_ss.at[e], x_rs.at[e], {"tensor": pt[e]}))
    zs += [send_gate(e) for e in range(early, nt)]

    def put_own(lanes, val):
        x_all[own_rows, lanes] = val

    conv_group(0, put_own)
    e_s[...] = (iota((128, LW), 1) // HS == iota((128, LW), 0)).astype(F32)
    spread16 = e_s[...].astype(BF)

    def spread(rows):
        return dot(jnp.broadcast_to(rows, (8, 128)), e_s[...], precision=HI)

    for cp in dts:
        cp.wait()
    HR = at_s.shape[1]
    HA = dt_ref.shape[0]
    sel = ((iota((HA, 128), 0) == iota((HA, 128), 1) + t * hl) & (iota((HA, 128), 1) < hl)).astype(BF)
    sel_t = ((iota((HR, HA), 1) == iota((HR, HA), 0) + t * hl) & (iota((HR, HA), 0) < hl)).astype(BF)
    eye = (iota((HR, 128), 0) == iota((HR, 128), 1)).astype(F32)
    place_head = (iota((hl, 128), 0) == iota((hl, 128), 1)).astype(F32)
    hp = [
        dot(jnp.broadcast_to(v[...], (8, hl)), place_head, precision=HI)[0:1, :] for v in (sb_ref, dr_ref, sk_ref)
    ]
    hp_t = [dot(eye, jnp.broadcast_to(v, (8, 128)), 1, 1, HI)[:, 0:1] for v in hp[0:2]]
    tri = (iota((L, L), 0) >= iota((L, L), 1)).astype(F32)

    def softplus(v):
        return jnp.maximum(v, 0.0) + jnp.log1p(jnp.exp(-jnp.abs(v)))

    for b in range(nt):
        rows = slice(b * L, (b + 1) * L)
        raw = dt_all[b]
        step = softplus(dot(raw, sel, 0, 0) + hp[0])
        step_s[rows, :] = step
        a_s[rows, :] = dot(tri, -step * jnp.exp(hp[1]), precision=HI)
        step_t = softplus(dot(sel_t, raw) + hp_t[0])
        stept_s[b] = step_t
        at_s[b] = dot(-step_t * jnp.exp(hp_t[1]), tri, 1, 1, HI)
    cu = dot(up_ref[...], cot_ref[...], 1, 1)
    for ch in range(len(chunks)):
        w_arrive(0, ch)
    for cp in bcs:
        cp.wait()
    for cp in xs:
        cp.wait()

    state = jnp.zeros((N, LW), F32)
    before = jnp.zeros((1, 128), F32)
    for b in range(nt):
        rows = slice(b * L, (b + 1) * L)
        stl[b, 0:N, :] = state
        stl[b, N : N + 8, :] = spread(jnp.exp(before))
        a = a_s[rows, :]
        last = a[L - 1 : L, :]
        weight = (jnp.exp(last - a) * step_s[rows, :]).astype(BF)
        xw = (x_all[rows, :].astype(F32) * dot(weight, spread16)).astype(BF)
        state = spread(jnp.exp(last))[0:1, :] * state + dot(bc_all[rows, 0:N], xw, 0, 0)
        before = before + last
    msg[0:N, :] = state
    msg[N : N + 8, :] = spread(before)
    sts = [
        copy(msg, st_in.at[c], st_ss.at[k], st_rs.at[k], {"context": lax.rem(c + k, nc)})
        for k in range(1, nc)
    ]

    left = iota((L, 2 * HS), 1) < HS

    def inner(b, carry):
        rows = pl.ds(pl.multiple_of(b * L, L), L)
        gram = dot(bc_all[rows, N : 2 * N], bc_all[rows, 0:N], 1, 1)
        gram = jnp.where(iota((L, L), 0) >= iota((L, L), 1), gram, 0.0)
        a = a_s[rows, :]
        at = at_s[b]
        stt = stept_s[b]
        for pair in range(hl // 2):
            lanes = slice(pair * 2 * HS, (pair + 1) * 2 * HS)
            xp = x_all[rows, lanes]
            out = []
            for h in (2 * pair, 2 * pair + 1):
                gap = jnp.minimum(a[:, h : h + 1] - at[h : h + 1, :], 0.0)
                m = (jnp.exp(gap) * gram * stt[h : h + 1, :]).astype(BF)
                out.append(dot(m, xp))
            y_s[rows, lanes] = jnp.where(left, out[0], out[1])
        return carry

    lax.fori_loop(0, nt, inner, 0)

    for cp in sts:
        cp.wait()
    inc_s[...] = jnp.zeros_like(inc_s)

    def chain(k, carry):
        inc_s[...] = jnp.exp(st_in[k, N : N + 1, :]) * inc_s[...] + st_in[k, 0:N, :]
        return carry

    lax.fori_loop(0, c, chain, 0)
    own_w.wait()
    skip = spread(hp[2])[0:1, :]
    ones = jnp.ones((8, LW), BF)

    def scatter(unit, b, cols):
        return remote(
            rs_send.at[pl.ds(pl.multiple_of(b * L, L), L), cols], rs_recv.at[t, :, cols],
            r_ss.at[unit, b], r_rs.at[unit, t], {"tensor": b},
        )

    def scattered(unit, b, cols):
        return remote(
            rs_send.at[pl.ds(pl.multiple_of(b * L, L), L), cols], rs_recv.at[b, :, cols],
            r_ss.at[unit, b], r_rs.at[unit, b], {"tensor": b},
        )

    units = [(0, None, 0, W)] + [(s, ch) + chunks[ch] for s in range(1, nf) for ch in range(len(chunks))]
    spans = [pl.ds(pl.multiple_of(order[s] * W + off, 128), wide) for s, _, off, wide in units]

    def gate(e, carry):
        b = peer(e)
        rows = pl.ds(pl.multiple_of(b * L, L), L)

        @pl.when(e == 0)
        def _():
            own_z.wait()

        @pl.when(e > 0)
        def _():
            remote(
                z_ref.at[:, own_cols], z_all.at[rows, :], z_ss.at[e], z_rs.at[e], {"tensor": b}
            ).wait_recv()

        start = (stl[b, 0:N, :] + stl[b, N : N + 1, :] * inc_s[...]).astype(BF)
        reach = dot(jnp.exp(a_s[rows, :]).astype(BF), spread16)
        y = y_s[rows, :] + reach * dot(bc_all[rows, N : 2 * N], start)
        y = y + skip * x_all[rows, :].astype(F32)
        z = z_all[rows, :].astype(F32)
        g = y * (z / (1.0 + jnp.exp(-z)))
        out = (g * gain_ref[...]).astype(BF)
        g_s[rows, :] = out
        adx[b, 0:16, :] = dot(down_ref[...], out, 1, 1)
        adx[b, 16:24, :] = dot(ones, (g * g).astype(BF), 1, 1)

        @pl.when(e > 0)
        def _():
            remote(adx.at[b], ad_in.at[e], ad_ss.at[e], ad_rs.at[e], {"tensor": b}).start()

        rs_send[rows, spans[0]] = dot(out, wbuf[f]).astype(BF)

        @pl.when(e > 0)
        def _():
            scatter(0, b, spans[0]).start()

        return carry

    lax.fori_loop(0, nt, gate, 0)

    half = (nt * L) // 2

    def project(u):
        slot, ch, off, wide = units[u]
        w_ready(slot, ch)

        def lap(i, carry):
            rows = pl.ds(pl.multiple_of(i * half, half), half)
            rs_send[rows, spans[u]] = dot(g_s[rows, :], wbuf[order[slot], :, off : off + wide]).astype(BF)
            for j in range(half // L):
                b = i * (half // L) + j

                @pl.when(b != t)
                def _():
                    scatter(u, b, spans[u]).start()

            return carry

        lax.fori_loop(0, 2, lap, 0)

    nch = len(chunks)
    if steps > 1:
        w_arrive(1, 0)
    for ch in range(nch):
        project(1 + ch)
    for e in range(1, nt):
        remote(adx.at[pt[e]], ad_in.at[e], ad_ss.at[e], ad_rs.at[e], {"tensor": pt[e]}).wait()
    red = adx[t]
    for e in range(1, nt):
        red = red + ad_in[e]
    scale_row = lax.rsqrt(red[16:17, :] / (LW * nt) + EPS)
    ad16 = red[0:16, :].astype(BF)
    factor = 2.0 / math.sqrt(L * nt * nc * nf)
    ag_own[...] = (factor * scale_row * cu).astype(BF)
    ags = [copy(ag_own, ag_all.at[t], ag_ss.at[e], ag_rs.at[e], {"tensor": pt[e]}) for e in range(1, nt)]
    gb_own[...] = dot((factor * scale_row * ad16.astype(F32)).astype(BF), cot_ref[...]).astype(BF)
    part = gb_own.shape[1] // nt
    own_part = pl.ds(pl.multiple_of(t * part, 128), part)
    gbs = [
        copy(
            gb_own.at[:, pl.ds(pl.multiple_of(pt[e] * part, 128), part)],
            gb_in.at[e], ga_ss.at[e], ga_rs.at[e], {"tensor": pt[e]},
        )
        for e in range(1, nt)
    ]
    scale_col = dot(jnp.broadcast_to(scale_row, (8, L)), jnp.full((8, 128), 0.125, F32), 0, 0, HI)[:, 0:1]
    for s in range(1, steps):
        for ch in range(nch):
            if s > 1 or ch > 0:
                if s == 1:
                    w_arrive(s, ch)
    for s in range(2, nf - 1):
        if s > 2:
            for ch in range(nch):
                w_arrive(s - 1, ch)
        for ch in range(nch):
            project(1 + (s - 1) * nch + ch)
    for cp in ags + gbs:
        cp.wait()
    ag_all[t] = ag_own[...]
    grad = jnp.zeros((16, LW), F32)
    for s in range(nt):
        grad = grad + dot(ag_all[s], g_s[s * L : (s + 1) * L, :])
    comb[:, 0:LW] = grad
    acc = gb_own[:, own_part].astype(F32)
    for e in range(1, nt):
        acc = acc + gb_in[e].astype(F32)
    comb[:, LW : LW + part] = acc
    lanes = (LW + part) // 128
    per = -(-lanes // nc)

    def seg(i):
        return pl.ds(pl.multiple_of(jnp.minimum(i * per, lanes - per) * 128, 128), per * 128)

    ccs = [
        copy(comb.at[:, seg(lax.rem(c + k, nc))], comb_c.at[k], cc_ss.at[k], cc_rs.at[k], {"context": lax.rem(c + k, nc)})
        for k in range(1, nc)
    ]
    if steps > 2:
        w_arrive(steps - 1, 0)
    for cp in ccs:
        cp.wait()
    acc = comb[:, seg(c)]
    for k in range(1, nc):
        acc = acc + comb_c[k]
    comb2[...] = acc.astype(BF)
    cfs = [copy(comb2, comb_f.at[f], cf_ss.at[k], cf_rs.at[k], {"fsdp": lax.rem(f + k, nf)}) for k in range(1, nf)]
    comb_f[f] = comb2[...]
    last = nf - 1
    if last > 1:
        project(1 + (last - 1) * nch)
        for ch in range(1, nch):
            if steps > 2:
                w_arrive(steps - 1, ch)
            project(1 + (last - 1) * nch + ch)

    def finish(u):
        slot, ch, off, wide = units[u]
        for e in range(1, nt):
            scattered(u, pt[e], spans[u]).wait()
        acc = rs_send[own_rows, spans[u]].astype(F32)
        for e in range(1, nt):
            acc = acc + rs_recv[pt[e], :, spans[u]].astype(F32)
        acc = acc + 2.0 * dot(ad16, up_ref[:, spans[u]], 0, 0)
        mixed_ref[:, spans[u]] = (scale_col * acc).astype(BF)

    finish(0)
    for ch in range(nch):
        finish(1 + ch)
    for cp in cfs:
        cp.wait()
    acc = comb_f[0].astype(F32)
    for k in range(1, nf):
        acc = acc + comb_f[k].astype(F32)
    seg_own[...] = acc
    sgs = [copy(seg_own, seg_in.at[c], sg_ss.at[k], sg_rs.at[k], {"context": lax.rem(c + k, nc)}) for k in range(1, nc)]
    seg_in[c] = acc
    for cp in sgs:
        cp.wait()
    for i in range(nc):
        full[:, seg(i)] = seg_in[i]
    ga_ref[...] = full[:, 0:LW]
    fin[t] = full[:, LW : LW + part]
    fins = [copy(fin.at[t], fin.at[t], fin_ss.at[e], fin_rs.at[e], {"tensor": pt[e]}) for e in range(1, nt)]
    for u in range(1 + nch, len(units)):
        finish(u)
    for cp in fins:
        cp.wait()
    for s in range(nt):
        gb_ref[:, s * part : (s + 1) * part] = fin[s]
    for cp in zs:
        cp.wait_send()
    for ch in range(nch):
        for s in range(steps):
            for dr in range(2):
                @pl.when(sends(dr, s))
                def _(dr=dr, s=s, ch=ch):
                    w_copy(dr, s, ch, f - s if dr == 0 else f + s).wait_send()

                @pl.when(gets(dr, s))
                def _(dr=dr, s=s, ch=ch):
                    for k in range(1, nc):
                        w_share(dr, s, ch, came(dr, s), k).wait_send()


def shards(x, bc, z, dt, taps, bias, step_bias, rate, skip, gain, w, down, up, cot):
    nt, nf, nc = lax.axis_size("tensor"), lax.axis_size("fsdp"), lax.axis_size("context")
    L, full = x.shape[1], x.shape[2]
    LW, hl, W, M = gain.shape[0], step_bias.shape[0], w.shape[1], cot.shape[2]
    BC = bc.shape[2]
    N = BC // 2
    HR = -(-hl // 8) * 8
    T = nt * L
    part = M // nt
    dt = dt[0].T
    down = down.T
    nch = len(column_chunks(W))
    units = 1 + (nf - 1) * nch
    lanes = (LW + part) // 128
    SW = -(-lanes // nc) * 128
    vm = pl.BlockSpec(memory_space=pltpu.VMEM)
    hbm = pl.BlockSpec(memory_space=pl.ANY)
    V = pltpu.VMEM
    D = pltpu.SemaphoreType.DMA
    scratch = [
        V((L, full), BF), V((L, BC), BF), V(dt.shape, BF), V(taps.shape, F32), V((1, full + BC), F32), V((1, LW), F32),
        V(down.shape, BF), V(up.shape, BF), V((L, M), BF),
        V((HALO, full), BF), V((HALO, BC), BF), V((nt - 1, L, LW), BF), V((T, LW), BF), V((T, LW), BF),
        V((T, BC), BF), V((nt,) + dt.shape, BF), V((nf, LW, W), BF), V((T, 128), F32), V((T, 128), F32),
        V((nt, HR, L), F32), V((nt, HR, L), F32),
        V((nt, N + 8, LW), F32), V((N + 8, LW), F32), V((nc, N + 8, LW), F32), V((N, LW), F32),
        V((128, LW), F32), V((T, LW), F32), V((T, LW), BF), V((nt, 24, L), F32), V((nt, 24, L), F32),
        V((16, L), BF), V((nt, 16, L), BF), V((16, M), BF), V((nt, 16, part), BF),
        V((16, LW + part), F32), V((nc, 16, SW), F32), V((16, SW), BF), V((nf, 16, SW), BF),
        V((16, SW), F32), V((nc, 16, SW), F32), V((16, LW + part), F32),
        V((nt, 16, part), F32), V((T, M), BF), V((nt, L, M), BF),
        D((9,)), D((2,)), D((2,)), D((nt,)), D((nt,)), D((nt,)), D((nt,)), D((nt,)), D((nt,)), D((nt,)), D((nt,)),
        D((2, nf - 1, nch)), D((2, nf - 1, nch)), D((2, nf - 1, nch, nc)), D((2, nf - 1, nch, nc)), D((nc,)), D((nc,)),
        D((nt,)), D((nt,)), D((nt,)), D((nt,)), D((nt,)), D((nt,)), D((nc,)), D((nc,)), D((nf,)), D((nf,)),
        D((nc,)), D((nc,)), D((nt,)), D((nt,)), D((units, nt)), D((units, nt)), D((2,)),
    ]
    mixed, ga, gb = pl.pallas_call(
        functools.partial(kernel, nt, nf, nc, hl),
        out_shape=(
            jax.ShapeDtypeStruct((L, M), BF),
            jax.ShapeDtypeStruct((16, LW), F32),
            jax.ShapeDtypeStruct((16, M), F32),
        ),
        in_specs=[hbm, hbm, hbm, hbm, hbm, hbm, vm, vm, vm, hbm, hbm, hbm, hbm, hbm],
        out_specs=(vm, vm, vm),
        scratch_shapes=scratch,
        compiler_params=pltpu.CompilerParams(
            collective_id=0, has_side_effects=True, vmem_limit_bytes=62 * 1024 * 1024
        ),
    )(x[0], bc[0], z[0], dt, taps, bias[None], step_bias[None], rate[None], skip[None], gain[None], w, down, up, cot[0])
    return mixed[None], ga.T, gb


def solution(mesh):
    tokens = P("fsdp", ("context", "tensor"), None)
    placed = (
        tokens, tokens, tokens, tokens, P(), P(), P("tensor"), P("tensor"), P("tensor"), P("tensor"),
        P("tensor", "fsdp"), P("tensor", None), P(), tokens,
    )
    return jax.shard_map(
        shards, mesh=mesh, in_specs=placed, out_specs=(tokens, P("tensor", None), P()), check_vma=False
    )
```

time: 116 us -> 90.5 us (0.78)
  the two profiles are of different devices: /device:TPU:24 before, /device:TPU:0 now
where the time goes in v1:
time: 90.5 us; the launch traced here: 90.3 us
  Pallas kernels  83.6 us (92%)
  local copies, waits for them, and re-layouts  5.97 us (7%)
    pallas_call x1, Pallas kernels, shards(): pl.pallas_call(functools.partial(kernel, nt, nf, nc, hl), out_shape=(jax....  83.6 us
    unnamed x7, local copies, waits for them, and re-layouts  3.32 us

profile of v1, /device:TPU:0, one launch (start us, length us, event | category | flops | bytes accessed | tf_op | source)
XLA Modules:
  0.0 90.3 jit_solution(13846768156930134783)
XLA Ops:
  0.6 1.3 %broadcast_in_dim.22.gain_hbm = f32[1,1280]{1,0:T(1,128)} reshape(f32[1280]{0:T(1024)} %param.23) | data formatting | bytes 10240 | tf_op jit(solution)/shard_map/broadcast_in_dim | solution.py:571
  1.9 1.4 %broadcast_in_dim.18.bias_hbm = f32[1,5376]{1,0:T(1,128)} reshape(f32[5376]{0:T(1024)} %param.19) | data formatting | bytes 43008 | tf_op jit(solution)/shard_map/broadcast_in_dim | solution.py:571
  3.3 83.6 %shard_map.157 = (bf16[128,2560]{1,0:T(8,128)(2,1)}, f32[16,1280]{1,0:T(8,128)}, f32[16,2560]{1,0:T(8,128)}) custom-call(bf16[128,5120]{1,0:T(8,128)(2,1)} %bitcast.13, bf16[128,256]{1,0:T(8,128)(2,1)} %bitcast.18, bf16[128,5120]{1,0:T(8,128)(2,1)} %bitcast.14, bf16[80,128]{1,0:T(8,128)(2,1)} %bitcast.20, f32[4,5376]{1,0:T(4,128)} %taps_hbm.1, ...), custom_call_target="tpu_custom_call" | custom-call | tf_op jit(solution)/shard_map/pallas_call | solution.py:558
  86.9 0.0 copy-start.1
  86.9 0.0 copy-start
  86.9 2.0 %copy.20 = bf16[1,128,2560]{2,1,0:T(8,128)(2,1)} copy(bf16[1,128,2560]{2,1,0:T(8,128)(2,1)} %bitcast.15) | data formatting | bytes 1310720
  88.9 0.0 copy-done.1
  88.9 0.6 copy.21
  89.6 0.0 copy-done
  89.6 0.7 copy.22
Async XLA Ops:
  86.9 2.0 %copy-start.1 = (f32[16,1280]{1,0:T(8,128)S(1)}, f32[16,1280]{1,0:T(8,128)}, u32[]{:S(2)}) copy-start(f32[16,1280]{1,0:T(8,128)} %get-tuple-element.7) | copy-start | bytes 245764
  86.9 2.7 %copy-start = (f32[16,2560]{1,0:T(8,128)S(1)}, f32[16,2560]{1,0:T(8,128)}, u32[]{:S(2)}) copy-start(f32[16,2560]{1,0:T(8,128)} %get-tuple-element.14) | copy-start | bytes 491524

commit v2 on v1

--- a/solution.py
+++ b/solution.py
@@ -13,7 +13,7 @@
 HI = lax.Precision.HIGHEST
 BF = jnp.bfloat16
 F32 = jnp.float32
-HALO = 16
+HALO = 8
 
 
 def dot(a, b, ca=1, cb=0, precision=None):
@@ -45,7 +45,7 @@
     mixed_ref, ga_ref, gb_ref,
     x_ref, bc_ref, dt_ref, taps_ref, bias_ref, gain_ref, down_ref, up_ref, cot_ref,
     halo_x, halo_bc, x_send, x_all, z_all, bc_all, dt_all, wbuf, a_s, step_s, at_s, stept_s,
-    stl, msg, st_in, inc_s, e_s, y_s, g_s, adx, ad_in, ag_own, ag_all, gb_own, gb_in,
+    stl, loc_s, skip_s, msg, st_in, inc_s, e_s, y_s, g_s, adx, ad_in, ag_own, ag_all, gb_own, gb_in,
     comb, comb_c, comb2, comb_f, seg_own, seg_in, full, fin, rs_send, rs_recv,
     ld, h_ss, h_rs, dt_ss, dt_rs, bc_ss, bc_rs, x_ss, x_rs, z_ss, z_rs, w_ss, w_rs, wf_ss, wf_rs, st_ss, st_rs,
     ad_ss, ad_rs, ag_ss, ag_rs, ga_ss, ga_rs, cc_ss, cc_rs, cf_ss, cf_rs, sg_ss, sg_rs, fin_ss, fin_rs, r_ss, r_rs, loc,
@@ -190,7 +190,7 @@
         lanes = pl.ds(col, 128)
         wide = pl.ds(tap_col, 128)
         ext = jnp.concatenate([halo[HALO - 8 : HALO, lanes].astype(F32) * live, src[:, lanes].astype(F32)], axis=0)
-        acc = bias_ref[:, wide] + taps_ref[0:1, wide] * ext[5 : 5 + L]
+        acc = bias_ref[wide][None, :] + taps_ref[0:1, wide] * ext[5 : 5 + L]
         for k in range(1, 4):
             acc = acc + taps_ref[k : k + 1, wide] * ext[5 + k : 5 + k + L]
         return (acc / (1.0 + jnp.exp(-acc))).astype(BF)
@@ -214,14 +214,12 @@
 
         lax.fori_loop(0, LW // 128, lap, 0)
 
-    for e in range(nt - 1, 0, -1):
+    for e in range(1, nt):
         def put(lanes, val, e=e):
             x_send[e - 1, :, lanes] = val
 
         conv_group(e, put)
         xs.append(copy(x_send.at[e - 1], x_all.at[own_rows, :], x_ss.at[e], x_rs.at[e], {"tensor": pt[e]}))
-    zs += [send_gate(e) for e in range(early, nt)]
-
     def put_own(lanes, val):
         x_all[own_rows, lanes] = val
 
@@ -258,40 +256,29 @@
         step_t = softplus(dot(sel_t, raw) + hp_t[0])
         stept_s[b] = step_t
         at_s[b] = dot(-step_t * jnp.exp(hp_t[1]), tri, 1, 1, HI)
-    cu = dot(up_ref[...], cot_ref[...], 1, 1)
-    for ch in range(len(chunks)):
-        w_arrive(0, ch)
-    for cp in bcs:
-        cp.wait()
-    for cp in xs:
-        cp.wait()
-
-    state = jnp.zeros((N, LW), F32)
     before = jnp.zeros((1, 128), F32)
     for b in range(nt):
-        rows = slice(b * L, (b + 1) * L)
-        stl[b, 0:N, :] = state
+        last = a_s[(b + 1) * L - 1 : (b + 1) * L, :]
         stl[b, N : N + 8, :] = spread(jnp.exp(before))
+        loc_s[b, N : N + 8, :] = spread(jnp.exp(last))
+        before = before + last
+    msg[N : N + 8, :] = spread(before)
+    skip_s[...] = spread(hp[2])
+    cu = dot(up_ref[...], cot_ref[...], 1, 1)
+    left = iota((L, 2 * HS), 1) < HS
+
+    def spans_of(e):
+        b = pt[e]
+        rows = pl.ds(pl.multiple_of(b * L, L), L)
+        if e > 0:
+            bcs[e - 1].wait_recv()
+            xs[e - 1].wait_recv()
         a = a_s[rows, :]
-        last = a[L - 1 : L, :]
-        weight = (jnp.exp(last - a) * step_s[rows, :]).astype(BF)
+        weight = (jnp.exp(a[L - 1 : L, :] - a) * step_s[rows, :]).astype(BF)
         xw = (x_all[rows, :].astype(F32) * dot(weight, spread16)).astype(BF)
-        state = spread(jnp.exp(last))[0:1, :] * state + dot(bc_all[rows, 0:N], xw, 0, 0)
-        before = before + last
-    msg[0:N, :] = state
-    msg[N : N + 8, :] = spread(before)
-    sts = [
-        copy(msg, st_in.at[c], st_ss.at[k], st_rs.at[k], {"context": lax.rem(c + k, nc)})
-        for k in range(1, nc)
-    ]
-
-    left = iota((L, 2 * HS), 1) < HS
-
-    def inner(b, carry):
-        rows = pl.ds(pl.multiple_of(b * L, L), L)
+        loc_s[b, 0:N, :] = dot(bc_all[rows, 0:N], xw, 0, 0)
         gram = dot(bc_all[rows, N : 2 * N], bc_all[rows, 0:N], 1, 1)
         gram = jnp.where(iota((L, L), 0) >= iota((L, L), 1), gram, 0.0)
-        a = a_s[rows, :]
         at = at_s[b]
         stt = stept_s[b]
         for pair in range(hl // 2):
@@ -303,10 +290,34 @@
                 m = (jnp.exp(gap) * gram * stt[h : h + 1, :]).astype(BF)
                 out.append(dot(m, xp))
             y_s[rows, lanes] = jnp.where(left, out[0], out[1])
-        return carry
-
-    lax.fori_loop(0, nt, inner, 0)
-
+
+    for e in range(nt):
+
+        spans_of(e)
+        if e == 0:
+            w_arrive(0, 0)
+        if e == min(1, nt - 2):
+            for ch in range(1, len(chunks)):
+                w_arrive(0, ch)
+        if e == nt - 2:
+            for cp in xs:
+                cp.wait_send()
+            zs += [send_gate(i) for i in range(early, nt)]
+    for cp in bcs:
+        cp.wait_send()
+
+    state = jnp.zeros((N, LW), F32)
+    for b in range(nt):
+        stl[b, 0:N, :] = state
+        state = loc_s[b, N : N + 1, :] * state + loc_s[b, 0:N, :]
+    msg[0:N, :] = state
+    sts = [
+        copy(msg, st_in.at[c], st_ss.at[k], st_rs.at[k], {"context": lax.rem(c + k, nc)})
+        for k in range(1, nc)
+    ]
+
+    if steps > 1:
+        w_arrive(1, 0)
     for cp in sts:
         cp.wait()
     inc_s[...] = jnp.zeros_like(inc_s)
@@ -317,7 +328,7 @@
 
     lax.fori_loop(0, c, chain, 0)
     own_w.wait()
-    skip = spread(hp[2])[0:1, :]
+    skip = skip_s[0:1, :]
     ones = jnp.ones((8, LW), BF)
 
     def scatter(unit, b, cols):
@@ -334,6 +345,8 @@
 
     units = [(0, None, 0, W)] + [(s, ch) + chunks[ch] for s in range(1, nf) for ch in range(len(chunks))]
     spans = [pl.ds(pl.multiple_of(order[s] * W + off, 128), wide) for s, _, off, wide in units]
+
+    held = max(nt - 1, 1)
 
     def gate(e, carry):
         b = peer(e)
@@ -355,7 +368,7 @@
         y = y + skip * x_all[rows, :].astype(F32)
         z = z_all[rows, :].astype(F32)
         g = y * (z / (1.0 + jnp.exp(-z)))
-        out = (g * gain_ref[...]).astype(BF)
+        out = (g * gain_ref[...][None, :]).astype(BF)
         g_s[rows, :] = out
         adx[b, 0:16, :] = dot(down_ref[...], out, 1, 1)
         adx[b, 16:24, :] = dot(ones, (g * g).astype(BF), 1, 1)
@@ -366,7 +379,7 @@
 
         rs_send[rows, spans[0]] = dot(out, wbuf[f]).astype(BF)
 
-        @pl.when(e > 0)
+        @pl.when((e > 0) & (e < held))
         def _():
             scatter(0, b, spans[0]).start()
 
@@ -376,19 +389,20 @@
 
     half = (nt * L) // 2
 
-    def project(u):
+    def project(u, send=True):
         slot, ch, off, wide = units[u]
         w_ready(slot, ch)
 
         def lap(i, carry):
             rows = pl.ds(pl.multiple_of(i * half, half), half)
             rs_send[rows, spans[u]] = dot(g_s[rows, :], wbuf[order[slot], :, off : off + wide]).astype(BF)
-            for j in range(half // L):
-                b = i * (half // L) + j
-
-                @pl.when(b != t)
-                def _():
-                    scatter(u, b, spans[u]).start()
+            if send:
+                for j in range(half // L):
+                    b = i * (half // L) + j
+
+                    @pl.when(b != t)
+                    def _():
+                        scatter(u, b, spans[u]).start()
 
             return carry
 
@@ -396,9 +410,10 @@
 
     nch = len(chunks)
     if steps > 1:
-        w_arrive(1, 0)
+        for ch in range(1, nch):
+            w_arrive(1, ch)
     for ch in range(nch):
-        project(1 + ch)
+        project(1 + ch, send=False)
     for e in range(1, nt):
         remote(adx.at[pt[e]], ad_in.at[e], ad_ss.at[e], ad_rs.at[e], {"tensor": pt[e]}).wait()
     red = adx[t]
@@ -419,12 +434,12 @@
         )
         for e in range(1, nt)
     ]
+    for e in range(held, nt):
+        scatter(0, pt[e], spans[0]).start()
+    for ch in range(nch):
+        for e in range(1, nt):
+            scatter(1 + ch, pt[e], spans[1 + ch]).start()
     scale_col = dot(jnp.broadcast_to(scale_row, (8, L)), jnp.full((8, 128), 0.125, F32), 0, 0, HI)[:, 0:1]
-    for s in range(1, steps):
-        for ch in range(nch):
-            if s > 1 or ch > 0:
-                if s == 1:
-                    w_arrive(s, ch)
     for s in range(2, nf - 1):
         if s > 2:
             for ch in range(nch):
@@ -517,6 +532,17 @@
                 def _(dr=dr, s=s, ch=ch):
                     for k in range(1, nc):
                         w_share(dr, s, ch, came(dr, s), k).wait_send()
+
+
+def write_out(mixed, ga, gb, mixed_out, ga_out, gb_out, sem):
+    copies = [
+        pltpu.make_async_copy(src, dst, sem.at[i])
+        for i, (src, dst) in enumerate(((mixed, mixed_out), (ga, ga_out), (gb, gb_out)))
+    ]
+    for cp in copies:
+        cp.start()
+    for cp in copies:
+        cp.wait()
 
 
 def shards(x, bc, z, dt, taps, bias, step_bias, rate, skip, gain, w, down, up, cot):
@@ -539,12 +565,12 @@
     V = pltpu.VMEM
     D = pltpu.SemaphoreType.DMA
     scratch = [
-        V((L, full), BF), V((L, BC), BF), V(dt.shape, BF), V(taps.shape, F32), V((1, full + BC), F32), V((1, LW), F32),
+        V((L, full), BF), V((L, BC), BF), V(dt.shape, BF), V(taps.shape, F32), V((full + BC,), F32), V((LW,), F32),
         V(down.shape, BF), V(up.shape, BF), V((L, M), BF),
         V((HALO, full), BF), V((HALO, BC), BF), V((nt - 1, L, LW), BF), V((T, LW), BF), V((T, LW), BF),
         V((T, BC), BF), V((nt,) + dt.shape, BF), V((nf, LW, W), BF), V((T, 128), F32), V((T, 128), F32),
         V((nt, HR, L), F32), V((nt, HR, L), F32),
-        V((nt, N + 8, LW), F32), V((N + 8, LW), F32), V((nc, N + 8, LW), F32), V((N, LW), F32),
+        V((nt, N + 8, LW), F32), V((nt, N + 8, LW), F32), V((8, LW), F32), V((N + 8, LW), F32), V((nc, N + 8, LW), F32), V((N, LW), F32),
         V((128, LW), F32), V((T, LW), F32), V((T, LW), BF), V((nt, 24, L), F32), V((nt, 24, L), F32),
         V((16, L), BF), V((nt, 16, L), BF), V((16, M), BF), V((nt, 16, part), BF),
         V((16, LW + part), F32), V((nc, 16, SW), F32), V((16, SW), BF), V((nf, 16, SW), BF),
@@ -557,18 +583,26 @@
     ]
     mixed, ga, gb = pl.pallas_call(
         functools.partial(kernel, nt, nf, nc, hl),
-        out_shape=(
-            jax.ShapeDtypeStruct((L, M), BF),
-            jax.ShapeDtypeStruct((16, LW), F32),
-            jax.ShapeDtypeStruct((16, M), F32),
-        ),
+        out_shape=(V((L, M), BF), V((16, LW), F32), V((16, M), F32)),
         in_specs=[hbm, hbm, hbm, hbm, hbm, hbm, vm, vm, vm, hbm, hbm, hbm, hbm, hbm],
         out_specs=(vm, vm, vm),
         scratch_shapes=scratch,
         compiler_params=pltpu.CompilerParams(
             collective_id=0, has_side_effects=True, vmem_limit_bytes=62 * 1024 * 1024
         ),
-    )(x[0], bc[0], z[0], dt, taps, bias[None], step_bias[None], rate[None], skip[None], gain[None], w, down, up, cot[0])
+    )(x[0], bc[0], z[0], dt, taps, bias, step_bias[None], rate[None], skip[None], gain, w, down, up, cot[0])
+    mixed, ga, gb = (pltpu.with_memory_space_constraint(v, pltpu.VMEM) for v in (mixed, ga, gb))
+    mixed, ga, gb = pl.pallas_call(
+        write_out,
+        out_shape=(
+            jax.ShapeDtypeStruct((L, M), BF),
+            jax.ShapeDtypeStruct((16, LW), F32),
+            jax.ShapeDtypeStruct((16, M), F32),
+        ),
+        in_specs=[vm, vm, vm],
+        out_specs=(hbm, hbm, hbm),
+        scratch_shapes=[D((3,))],
+    )(mixed, ga, gb)
     return mixed[None], ga.T, gb
 
 

time: 90.5 us -> 80.6 us (0.89)
  local copies, waits for them, and re-layouts: 5.97 us -> 0 us
  Pallas kernels: 83.6 us -> 79.8 us
    pallas_call x1 -> x2, Pallas kernels: 83.6 us -> 79.8 us  [the longest x1 78.9 us: shards(): pl.pallas_call(functools.partial(kernel, nt, nf, nc, hl), out_shape=(V((L...]
    unnamed x7 -> x0, local copies, waits for them, and re-layouts: 3.32 us -> none
    broadcast_in_dim x2 -> x0, local copies, waits for them, and re-layouts: 2.65 us -> none  [the longest x1 1.36 us: shards(): bias[None]]
where the time goes in v2:
time: 80.6 us; the launch traced here: 80.5 us
  Pallas kernels  79.8 us (99%)
    pallas_call x1, Pallas kernels, shards(): pl.pallas_call(functools.partial(kernel, nt, nf, nc, hl), out_shape=(V((L...  78.9 us

profile of v2, /device:TPU:0, one launch (start us, length us, event | category | flops | bytes accessed | tf_op | source)
XLA Modules:
  0.0 80.5 jit_solution(16275878595550937735)
XLA Ops:
  0.6 78.9 %shard_map.157 = (bf16[128,2560]{1,0:T(8,128)(2,1)S(1)}, f32[16,1280]{1,0:T(8,128)S(1)}, f32[16,2560]{1,0:T(8,128)S(1)}) custom-call(bf16[128,5120]{1,0:T(8,128)(2,1)} %bitcast.13, bf16[128,256]{1,0:T(8,128)(2,1)} %bitcast.16, bf16[128,5120]{1,0:T(8,128)(2,1)} %bitcast.14, bf16[80,128]{1,0:T(8,128)(2,1)} %bitcast.18, f32[4,5376]{1,0:T(4,128)} %taps_hbm.1, ...), custom_call_target="tpu_custom_call" | custom-call | tf_op jit(solution)/shard_map/pallas_call | solution.py:584
  79.5 0.9 %shard_map.158 = (bf16[128,2560]{1,0:T(8,128)(2,1)}, f32[16,1280]{1,0:T(8,128)}, f32[16,2560]{1,0:T(8,128)}) custom-call(bf16[128,2560]{1,0:T(8,128)(2,1)S(1)} %get-tuple-element.9.mixed, f32[16,1280]{1,0:T(8,128)S(1)} %get-tuple-element.10.ga, f32[16,2560]{1,0:T(8,128)S(1)} %get-tuple-element.11.gb), custom_call_target="tpu_custom_call" | custom-call | tf_op jit(solution)/shard_map/pallas_call | solution.py:595

commit v3 on v2

--- a/solution.py
+++ b/solution.py
@@ -31,6 +31,10 @@
     for k in range(1, len(values)):
         out = jnp.where(i == k, jnp.int32(values[k]), out)
     return out
+
+
+def grid_of(count):
+    return (2, count // 2) if count % 2 == 0 else (1, count)
 
 
 def column_chunks(width):
@@ -46,9 +50,9 @@
     x_ref, bc_ref, dt_ref, taps_ref, bias_ref, gain_ref, down_ref, up_ref, cot_ref,
     halo_x, halo_bc, x_send, x_all, z_all, bc_all, dt_all, wbuf, a_s, step_s, at_s, stept_s,
     stl, loc_s, skip_s, msg, st_in, inc_s, e_s, y_s, g_s, adx, ad_in, ag_own, ag_all, gb_own, gb_in,
-    comb, comb_c, comb2, comb_f, seg_own, seg_in, full, fin, rs_send, rs_recv,
+    comb, comb_c, comb2, comb_f, seg_own, seg_in, full, fin, rs_send, rs_xa, rs_yb, sum_a, in_a, sum_b, in_b,
     ld, h_ss, h_rs, dt_ss, dt_rs, bc_ss, bc_rs, x_ss, x_rs, z_ss, z_rs, w_ss, w_rs, wf_ss, wf_rs, st_ss, st_rs,
-    ad_ss, ad_rs, ag_ss, ag_rs, ga_ss, ga_rs, cc_ss, cc_rs, cf_ss, cf_rs, sg_ss, sg_rs, fin_ss, fin_rs, r_ss, r_rs, loc,
+    ad_ss, ad_rs, ag_ss, ag_rs, ga_ss, ga_rs, cc_ss, cc_rs, cf_ss, cf_rs, sg_ss, sg_rs, fin_ss, fin_rs, rs_ss, rs_rs, loc,
 ):
     t = lax.axis_index("tensor")
     f = lax.axis_index("fsdp")
@@ -84,6 +88,12 @@
             src_ref=src, dst_ref=dst, send_sem=ss, recv_sem=rs, device_id=dev, device_id_type=MESH
         )
 
+    def sent(region, sem):
+        remote(region, region, sem, sem, {"tensor": pt[nt - 1]}).wait_send()
+
+    def landed(region, sem):
+        remote(region, region, sem, sem, {"tensor": pt[nt - 1]}).wait_recv()
+
     def copy(src, dst, ss, rs, dev):
         cp = remote(src, dst, ss, rs, dev)
         cp.start()
@@ -119,18 +129,19 @@
 
     h1 = copy(x_ref.at[L - HALO : L, :], halo_x, h_ss.at[0], h_rs.at[0], place(nxt))
     h2 = copy(bc_ref.at[L - HALO : L, :], halo_bc, h_ss.at[1], h_rs.at[1], place(nxt))
-    dts = [copy(dt_ref, dt_all.at[t], dt_ss.at[e], dt_rs.at[e], {"tensor": pt[e]}) for e in range(1, nt)]
+    for e in range(1, nt):
+        copy(dt_ref, dt_all.at[t], dt_ss.at[0], dt_rs.at[0], {"tensor": pt[e]})
     share = pl.ds(pl.multiple_of(c * R, 16), R)
 
     def w_copy(dr, s, ch, q):
         cols = pl.ds(chunks[ch][0], chunks[ch][1])
         src = w_ref.at[share, cols] if s == 0 else wbuf.at[q, share, cols]
         to = f + 1 if dr == 0 else f - 1
-        return remote(src, wbuf.at[q, share, cols], w_ss.at[dr, s, ch], w_rs.at[dr, s, ch], {"fsdp": to})
+        return remote(src, wbuf.at[q, share, cols], w_ss.at[dr, s], w_rs.at[dr, s, ch], {"fsdp": to})
 
     def w_share(dr, s, ch, q, k):
         region = wbuf.at[q, share, pl.ds(chunks[ch][0], chunks[ch][1])]
-        return remote(region, region, wf_ss.at[dr, s, ch, k], wf_rs.at[dr, s, ch, k], {"context": lax.rem(c + k, nc)})
+        return remote(region, region, wf_ss.at[dr, s], wf_rs.at[dr, s, ch], {"context": lax.rem(c + k, nc)})
 
     def has_next(dr):
         return f + 1 < nf if dr == 0 else f >= 1
@@ -169,19 +180,17 @@
     dist = [pick([max(abs(table[g][i] - g) - 1, 0) for g in range(nf)], f) for i in range(nf)]
 
     def w_ready(slot, ch):
-        region = wbuf.at[order[slot], share, pl.ds(chunks[ch][0], chunks[ch][1])]
-        for k in range(1, nc):
-            remote(
-                region, region, wf_ss.at[way[slot], dist[slot], ch, k], wf_rs.at[way[slot], dist[slot], ch, k],
-                {"context": lax.rem(c + k, nc)},
-            ).wait_recv()
+        region = wbuf.at[order[slot], 0 : (nc - 1) * R, pl.ds(chunks[ch][0], chunks[ch][1])]
+        if nc > 1:
+            landed(region, wf_rs.at[way[slot], dist[slot], ch])
 
     def send_gate(e):
         cols = pl.ds(pl.multiple_of(pt[e] * LW, 128), LW)
-        return copy(z_ref.at[:, cols], z_all.at[own_rows, :], z_ss.at[e], z_rs.at[e], {"tensor": pt[e]})
+        return copy(z_ref.at[:, cols], z_all.at[own_rows, :], z_ss.at[0], z_rs.at[e], {"tensor": pt[e]})
 
     early = nt - 1 if nt > 2 else nt
-    zs = [send_gate(e) for e in range(1, early)]
+    for e in range(1, early):
+        send_gate(e)
     h1.wait()
     h2.wait()
     live = (idx > 0).astype(F32)
@@ -199,7 +208,7 @@
     for j in range(2 * N // 128):
         bc_all[own_rows, j * 128 : (j + 1) * 128] = conv(bc_ref, halo_bc, j * 128, wide0 + j * 128)
     bcs = [
-        copy(bc_all.at[own_rows, :], bc_all.at[own_rows, :], bc_ss.at[e], bc_rs.at[e], {"tensor": pt[e]})
+        copy(bc_all.at[own_rows, :], bc_all.at[own_rows, :], bc_ss.at[0], bc_rs.at[e], {"tensor": pt[e]})
         for e in range(1, nt)
     ]
     xs = []
@@ -219,7 +228,7 @@
             x_send[e - 1, :, lanes] = val
 
         conv_group(e, put)
-        xs.append(copy(x_send.at[e - 1], x_all.at[own_rows, :], x_ss.at[e], x_rs.at[e], {"tensor": pt[e]}))
+        xs.append(copy(x_send.at[e - 1], x_all.at[own_rows, :], x_ss.at[0], x_rs.at[e], {"tensor": pt[e]}))
     def put_own(lanes, val):
         x_all[own_rows, lanes] = val
 
@@ -230,8 +239,7 @@
     def spread(rows):
         return dot(jnp.broadcast_to(rows, (8, 128)), e_s[...], precision=HI)
 
-    for cp in dts:
-        cp.wait()
+    landed(dt_all.at[0 : nt - 1], dt_rs.at[0])
     HR = at_s.shape[1]
     HA = dt_ref.shape[0]
     sel = ((iota((HA, 128), 0) == iota((HA, 128), 1) + t * hl) & (iota((HA, 128), 1) < hl)).astype(BF)
@@ -262,7 +270,7 @@
         stl[b, N : N + 8, :] = spread(jnp.exp(before))
         loc_s[b, N : N + 8, :] = spread(jnp.exp(last))
         before = before + last
-    msg[N : N + 8, :] = spread(before)
+    msg[N : N + 16, :] = jnp.broadcast_to(spread(jnp.exp(before))[0:1, :], (16, LW)).astype(BF)
     skip_s[...] = spread(hp[2])
     cu = dot(up_ref[...], cot_ref[...], 1, 1)
     left = iota((L, 2 * HS), 1) < HS
@@ -300,30 +308,26 @@
             for ch in range(1, len(chunks)):
                 w_arrive(0, ch)
         if e == nt - 2:
-            for cp in xs:
-                cp.wait_send()
-            zs += [send_gate(i) for i in range(early, nt)]
-    for cp in bcs:
-        cp.wait_send()
+            sent(x_send, x_ss.at[0])
+            for i in range(early, nt):
+                send_gate(i)
 
     state = jnp.zeros((N, LW), F32)
     for b in range(nt):
         stl[b, 0:N, :] = state
         state = loc_s[b, N : N + 1, :] * state + loc_s[b, 0:N, :]
-    msg[0:N, :] = state
+    msg[0:N, :] = state.astype(BF)
     sts = [
         copy(msg, st_in.at[c], st_ss.at[k], st_rs.at[k], {"context": lax.rem(c + k, nc)})
         for k in range(1, nc)
     ]
 
-    if steps > 1:
-        w_arrive(1, 0)
     for cp in sts:
         cp.wait()
     inc_s[...] = jnp.zeros_like(inc_s)
 
     def chain(k, carry):
-        inc_s[...] = jnp.exp(st_in[k, N : N + 1, :]) * inc_s[...] + st_in[k, 0:N, :]
+        inc_s[...] = st_in[k, N : N + 16, :].astype(F32)[0:1, :] * inc_s[...] + st_in[k, 0:N, :].astype(F32)
         return carry
 
     lax.fori_loop(0, c, chain, 0)
@@ -331,17 +335,63 @@
     skip = skip_s[0:1, :]
     ones = jnp.ones((8, LW), BF)
 
-    def scatter(unit, b, cols):
+    nx, ny = grid_of(nt)
+    xi, yi = lax.rem(t, nx), lax.div(t, nx)
+    top, low = slice(0, L // 2), slice(L // 2, L)
+    xo = nx - 1 - xi
+
+    def to_x(u, by):
         return remote(
-            rs_send.at[pl.ds(pl.multiple_of(b * L, L), L), cols], rs_recv.at[t, :, cols],
-            r_ss.at[unit, b], r_rs.at[unit, t], {"tensor": b},
+            rs_send.at[by, xo, top, spans[u]], rs_xa.at[by, :, spans[u]], rs_ss.at[0], rs_rs.at[u, 0],
+            {"tensor": yi * nx + xo},
         )
 
-    def scattered(unit, b, cols):
+    def to_y(u, j, bx):
+        ty = lax.rem(yi + j, ny)
         return remote(
-            rs_send.at[pl.ds(pl.multiple_of(b * L, L), L), cols], rs_recv.at[b, :, cols],
-            r_ss.at[unit, b], r_rs.at[unit, b], {"tensor": b},
+            rs_send.at[ty, bx, low, spans[u]], rs_yb.at[ny - j - 1, bx, :, spans[u]], rs_ss.at[1], rs_rs.at[u, 1],
+            {"tensor": ty * nx + xi},
         )
+
+    def send_block(u, by, bx):
+        @pl.when(bx != xi)
+        def _():
+            to_x(u, by).start()
+
+        for j in range(1, ny):
+            @pl.when(lax.rem(yi + j, ny) == by)
+            def _(j=j):
+                to_y(u, j, bx).start()
+
+    def send_unit(u):
+        if nx > 1:
+            to_x(u, slice(None)).start()
+        for j in range(1, ny):
+            to_y(u, j, slice(None)).start()
+
+    def second(u):
+        cols = spans[u]
+        if nx > 1:
+            landed(rs_xa.at[:, :, cols], rs_rs.at[u, 0])
+        if ny > 1:
+            landed(rs_yb.at[:, :, :, cols], rs_rs.at[u, 1])
+        for j in range(1, ny):
+            ty = lax.rem(yi + j, ny)
+            acc = rs_send[ty, xi, top, cols].astype(F32)
+            if nx > 1:
+                acc = acc + rs_xa[ty, :, cols].astype(F32)
+            sum_a[j - 1, :, cols] = acc.astype(BF)
+            remote(
+                sum_a.at[j - 1, :, cols], in_a.at[ny - j - 1, :, cols], rs_ss.at[2], rs_rs.at[u, 2], {"tensor": ty * nx + xi}
+            ).start()
+        if nx > 1:
+            acc = rs_send[yi, xo, low, cols].astype(F32)
+            for j in range(1, ny):
+                acc = acc + rs_yb[j - 1, xo, :, cols].astype(F32)
+            sum_b[:, cols] = acc.astype(BF)
+            remote(
+                sum_b.at[:, cols], in_b.at[:, cols], rs_ss.at[3], rs_rs.at[u, 3], {"tensor": yi * nx + xo}
+            ).start()
 
     units = [(0, None, 0, W)] + [(s, ch) + chunks[ch] for s in range(1, nf) for ch in range(len(chunks))]
     spans = [pl.ds(pl.multiple_of(order[s] * W + off, 128), wide) for s, _, off, wide in units]
@@ -356,10 +406,15 @@
         def _():
             own_z.wait()
 
+        if steps > 1:
+            @pl.when(e == nt - 1)
+            def _():
+                w_arrive(1, 0)
+
         @pl.when(e > 0)
         def _():
             remote(
-                z_ref.at[:, own_cols], z_all.at[rows, :], z_ss.at[e], z_rs.at[e], {"tensor": b}
+                z_ref.at[:, own_cols], z_all.at[rows, :], z_ss.at[0], z_rs.at[e], {"tensor": b}
             ).wait_recv()
 
         start = (stl[b, 0:N, :] + stl[b, N : N + 1, :] * inc_s[...]).astype(BF)
@@ -375,47 +430,36 @@
 
         @pl.when(e > 0)
         def _():
-            remote(adx.at[b], ad_in.at[e], ad_ss.at[e], ad_rs.at[e], {"tensor": b}).start()
-
-        rs_send[rows, spans[0]] = dot(out, wbuf[f]).astype(BF)
+            remote(adx.at[b], ad_in.at[e], ad_ss.at[0], ad_rs.at[0], {"tensor": b}).start()
+
+        by, bx = lax.div(b, nx), lax.rem(b, nx)
+        rs_send[by, bx, :, spans[0]] = dot(out, wbuf[f]).astype(BF)
 
         @pl.when((e > 0) & (e < held))
         def _():
-            scatter(0, b, spans[0]).start()
+            send_block(0, by, bx)
 
         return carry
 
     lax.fori_loop(0, nt, gate, 0)
 
-    half = (nt * L) // 2
-
-    def project(u, send=True):
+    def project(u):
         slot, ch, off, wide = units[u]
         w_ready(slot, ch)
 
-        def lap(i, carry):
-            rows = pl.ds(pl.multiple_of(i * half, half), half)
-            rs_send[rows, spans[u]] = dot(g_s[rows, :], wbuf[order[slot], :, off : off + wide]).astype(BF)
-            if send:
-                for j in range(half // L):
-                    b = i * (half // L) + j
-
-                    @pl.when(b != t)
-                    def _():
-                        scatter(u, b, spans[u]).start()
-
+        def lap(by, carry):
+            rows = pl.ds(pl.multiple_of(by * (nx * L), L), nx * L)
+            out = dot(g_s[rows, :], wbuf[order[slot], :, off : off + wide]).astype(BF)
+            for bx in range(nx):
+                rs_send[by, bx, :, spans[u]] = out[bx * L : (bx + 1) * L]
             return carry
 
-        lax.fori_loop(0, 2, lap, 0)
+        lax.fori_loop(0, ny, lap, 0)
 
     nch = len(chunks)
-    if steps > 1:
-        for ch in range(1, nch):
-            w_arrive(1, ch)
     for ch in range(nch):
-        project(1 + ch, send=False)
-    for e in range(1, nt):
-        remote(adx.at[pt[e]], ad_in.at[e], ad_ss.at[e], ad_rs.at[e], {"tensor": pt[e]}).wait()
+        project(1 + ch)
+    landed(ad_in.at[1:nt], ad_rs.at[0])
     red = adx[t]
     for e in range(1, nt):
         red = red + ad_in[e]
@@ -423,31 +467,34 @@
     ad16 = red[0:16, :].astype(BF)
     factor = 2.0 / math.sqrt(L * nt * nc * nf)
     ag_own[...] = (factor * scale_row * cu).astype(BF)
-    ags = [copy(ag_own, ag_all.at[t], ag_ss.at[e], ag_rs.at[e], {"tensor": pt[e]}) for e in range(1, nt)]
+    for e in range(1, nt):
+        copy(ag_own, ag_all.at[t], ag_ss.at[0], ag_rs.at[0], {"tensor": pt[e]})
     gb_own[...] = dot((factor * scale_row * ad16.astype(F32)).astype(BF), cot_ref[...]).astype(BF)
     part = gb_own.shape[1] // nt
     own_part = pl.ds(pl.multiple_of(t * part, 128), part)
-    gbs = [
+    for e in range(1, nt):
         copy(
             gb_own.at[:, pl.ds(pl.multiple_of(pt[e] * part, 128), part)],
-            gb_in.at[e], ga_ss.at[e], ga_rs.at[e], {"tensor": pt[e]},
+            gb_in.at[e], ga_ss.at[0], ga_rs.at[0], {"tensor": pt[e]},
         )
-        for e in range(1, nt)
-    ]
     for e in range(held, nt):
-        scatter(0, pt[e], spans[0]).start()
+        send_block(0, lax.div(pt[e], nx), lax.rem(pt[e], nx))
     for ch in range(nch):
-        for e in range(1, nt):
-            scatter(1 + ch, pt[e], spans[1 + ch]).start()
+        send_unit(1 + ch)
     scale_col = dot(jnp.broadcast_to(scale_row, (8, L)), jnp.full((8, 128), 0.125, F32), 0, 0, HI)[:, 0:1]
+    if steps > 1:
+        for ch in range(1, nch):
+            w_arrive(1, ch)
     for s in range(2, nf - 1):
         if s > 2:
             for ch in range(nch):
                 w_arrive(s - 1, ch)
         for ch in range(nch):
             project(1 + (s - 1) * nch + ch)
-    for cp in ags + gbs:
-        cp.wait()
+            send_unit(1 + (s - 1) * nch + ch)
+    second(0)
+    landed(ag_all.at[0 : nt - 1], ag_rs.at[0])
+    landed(gb_in.at[1:nt], ga_rs.at[0])
     ag_all[t] = ag_own[...]
     grad = jnp.zeros((16, LW), F32)
     for s in range(nt):
@@ -467,71 +514,98 @@
         copy(comb.at[:, seg(lax.rem(c + k, nc))], comb_c.at[k], cc_ss.at[k], cc_rs.at[k], {"context": lax.rem(c + k, nc)})
         for k in range(1, nc)
     ]
-    if steps > 2:
-        w_arrive(steps - 1, 0)
+    for ch in range(nch):
+        second(1 + ch)
     for cp in ccs:
         cp.wait()
     acc = comb[:, seg(c)]
     for k in range(1, nc):
         acc = acc + comb_c[k]
     comb2[...] = acc.astype(BF)
-    cfs = [copy(comb2, comb_f.at[f], cf_ss.at[k], cf_rs.at[k], {"fsdp": lax.rem(f + k, nf)}) for k in range(1, nf)]
+    for k in range(1, nf):
+        copy(comb2, comb_f.at[f], cf_ss.at[0], cf_rs.at[0], {"fsdp": lax.rem(f + k, nf)})
     comb_f[f] = comb2[...]
-    last = nf - 1
-    if last > 1:
-        project(1 + (last - 1) * nch)
-        for ch in range(1, nch):
-            if steps > 2:
-                w_arrive(steps - 1, ch)
-            project(1 + (last - 1) * nch + ch)
-
     def finish(u):
-        slot, ch, off, wide = units[u]
-        for e in range(1, nt):
-            scattered(u, pt[e], spans[u]).wait()
-        acc = rs_send[own_rows, spans[u]].astype(F32)
-        for e in range(1, nt):
-            acc = acc + rs_recv[pt[e], :, spans[u]].astype(F32)
-        acc = acc + 2.0 * dot(ad16, up_ref[:, spans[u]], 0, 0)
-        mixed_ref[:, spans[u]] = (scale_col * acc).astype(BF)
+        cols = spans[u]
+        up_part = rs_send[yi, xi, top, cols].astype(F32)
+        low_part = rs_send[yi, xi, low, cols].astype(F32)
+        if nx > 1:
+            landed(in_b.at[:, cols], rs_rs.at[u, 3])
+            up_part = up_part + rs_xa[yi, :, cols].astype(F32)
+            low_part = low_part + in_b[:, cols].astype(F32)
+        if ny > 1:
+            landed(in_a.at[:, :, cols], rs_rs.at[u, 2])
+        for j in range(1, ny):
+            up_part = up_part + in_a[j - 1, :, cols].astype(F32)
+            low_part = low_part + rs_yb[j - 1, xi, :, cols].astype(F32)
+        acc = jnp.concatenate([up_part, low_part], axis=0) + 2.0 * dot(ad16, up_ref[:, cols], 0, 0)
+        mixed_ref[:, cols] = (scale_col * acc).astype(BF)
 
     finish(0)
+    for u in range(1 + nch, 1 + (nf - 2) * nch):
+        second(u)
     for ch in range(nch):
         finish(1 + ch)
-    for cp in cfs:
-        cp.wait()
+    last = 1 + (nf - 2) * nch
+    for ch in range(nch):
+        if steps > 2:
+            w_arrive(steps - 1, ch)
+        if nf > 2:
+            project(last + ch)
+            send_unit(last + ch)
+        if ch == 0:
+            for u in range(1 + nch, last):
+                finish(u)
+    if nf > 2:
+        for ch in range(nch - 1):
+            second(last + ch)
+    landed(comb_f.at[0 : nf - 1], cf_rs.at[0])
     acc = comb_f[0].astype(F32)
     for k in range(1, nf):
         acc = acc + comb_f[k].astype(F32)
     seg_own[...] = acc
     sgs = [copy(seg_own, seg_in.at[c], sg_ss.at[k], sg_rs.at[k], {"context": lax.rem(c + k, nc)}) for k in range(1, nc)]
     seg_in[c] = acc
+    if nf > 2:
+        second(last + nch - 1)
     for cp in sgs:
         cp.wait()
     for i in range(nc):
         full[:, seg(i)] = seg_in[i]
     ga_ref[...] = full[:, 0:LW]
     fin[t] = full[:, LW : LW + part]
-    fins = [copy(fin.at[t], fin.at[t], fin_ss.at[e], fin_rs.at[e], {"tensor": pt[e]}) for e in range(1, nt)]
-    for u in range(1 + nch, len(units)):
-        finish(u)
-    for cp in fins:
-        cp.wait()
+    for e in range(1, nt):
+        copy(fin.at[t], fin.at[t], fin_ss.at[0], fin_rs.at[0], {"tensor": pt[e]})
+    if nf > 2:
+        for ch in range(nch):
+            finish(last + ch)
+    landed(fin.at[0 : nt - 1], fin_rs.at[0])
     for s in range(nt):
         gb_ref[:, s * part : (s + 1) * part] = fin[s]
-    for cp in zs:
-        cp.wait_send()
-    for ch in range(nch):
-        for s in range(steps):
-            for dr in range(2):
-                @pl.when(sends(dr, s))
-                def _(dr=dr, s=s, ch=ch):
-                    w_copy(dr, s, ch, f - s if dr == 0 else f + s).wait_send()
-
+    sent(dt_all.at[0 : nt - 1], dt_ss.at[0])
+    sent(bc_all.at[0 : (nt - 1) * L, :], bc_ss.at[0])
+    sent(z_all.at[0 : (nt - 1) * L, :], z_ss.at[0])
+    sent(ad_in.at[1:nt], ad_ss.at[0])
+    sent(ag_all.at[0 : nt - 1], ag_ss.at[0])
+    sent(gb_in.at[1:nt], ga_ss.at[0])
+    sent(comb_f.at[0 : nf - 1], cf_ss.at[0])
+    sent(fin.at[0 : nt - 1], fin_ss.at[0])
+    if nx > 1:
+        sent(rs_xa, rs_ss.at[0])
+        sent(in_b, rs_ss.at[3])
+    if ny > 1:
+        sent(rs_yb, rs_ss.at[1])
+        sent(in_a, rs_ss.at[2])
+    for s in range(steps):
+        for dr in range(2):
+            @pl.when(sends(dr, s))
+            def _(dr=dr, s=s):
+                sent(wbuf.at[0, 0:R, :], w_ss.at[dr, s])
+
+            if nc > 1:
                 @pl.when(gets(dr, s))
-                def _(dr=dr, s=s, ch=ch):
-                    for k in range(1, nc):
-                        w_share(dr, s, ch, came(dr, s), k).wait_send()
+                def _(dr=dr, s=s):
+                    sent(wbuf.at[0, 0 : (nc - 1) * R, :], wf_ss.at[dr, s])
 
 
 def write_out(mixed, ga, gb, mixed_out, ga_out, gb_out, sem):
@@ -554,6 +628,8 @@
     HR = -(-hl // 8) * 8
     T = nt * L
     part = M // nt
+    nx, ny = grid_of(nt)
+    my = max(ny - 1, 1)
     dt = dt[0].T
     down = down.T
     nch = len(column_chunks(W))
@@ -570,16 +646,17 @@
         V((HALO, full), BF), V((HALO, BC), BF), V((nt - 1, L, LW), BF), V((T, LW), BF), V((T, LW), BF),
         V((T, BC), BF), V((nt,) + dt.shape, BF), V((nf, LW, W), BF), V((T, 128), F32), V((T, 128), F32),
         V((nt, HR, L), F32), V((nt, HR, L), F32),
-        V((nt, N + 8, LW), F32), V((nt, N + 8, LW), F32), V((8, LW), F32), V((N + 8, LW), F32), V((nc, N + 8, LW), F32), V((N, LW), F32),
+        V((nt, N + 8, LW), F32), V((nt, N + 8, LW), F32), V((8, LW), F32), V((N + 16, LW), BF), V((nc, N + 16, LW), BF), V((N, LW), F32),
         V((128, LW), F32), V((T, LW), F32), V((T, LW), BF), V((nt, 24, L), F32), V((nt, 24, L), F32),
         V((16, L), BF), V((nt, 16, L), BF), V((16, M), BF), V((nt, 16, part), BF),
         V((16, LW + part), F32), V((nc, 16, SW), F32), V((16, SW), BF), V((nf, 16, SW), BF),
         V((16, SW), F32), V((nc, 16, SW), F32), V((16, LW + part), F32),
-        V((nt, 16, part), F32), V((T, M), BF), V((nt, L, M), BF),
-        D((9,)), D((2,)), D((2,)), D((nt,)), D((nt,)), D((nt,)), D((nt,)), D((nt,)), D((nt,)), D((nt,)), D((nt,)),
-        D((2, nf - 1, nch)), D((2, nf - 1, nch)), D((2, nf - 1, nch, nc)), D((2, nf - 1, nch, nc)), D((nc,)), D((nc,)),
-        D((nt,)), D((nt,)), D((nt,)), D((nt,)), D((nt,)), D((nt,)), D((nc,)), D((nc,)), D((nf,)), D((nf,)),
-        D((nc,)), D((nc,)), D((nt,)), D((nt,)), D((units, nt)), D((units, nt)), D((2,)),
+        V((nt, 16, part), F32), V((ny, nx, L, M), BF), V((ny, L // 2, M), BF), V((my, nx, L // 2, M), BF),
+        V((my, L // 2, M), BF), V((my, L // 2, M), BF), V((L // 2, M), BF), V((L // 2, M), BF),
+        D((9,)), D((2,)), D((2,)), D((1,)), D((1,)), D((1,)), D((nt,)), D((1,)), D((nt,)), D((1,)), D((nt,)),
+        D((2, nf - 1)), D((2, nf - 1, nch)), D((2, nf - 1)), D((2, nf - 1, nch)), D((nc,)), D((nc,)),
+        D((1,)), D((1,)), D((1,)), D((1,)), D((1,)), D((1,)), D((nc,)), D((nc,)), D((1,)), D((1,)),
+        D((nc,)), D((nc,)), D((1,)), D((1,)), D((4,)), D((units, 4)), D((2,)),
     ]
     mixed, ga, gb = pl.pallas_call(
         functools.partial(kernel, nt, nf, nc, hl),

time: 80.6 us -> 77.2 us (0.958)
  Pallas kernels: 79.8 us -> 76.4 us
    pallas_call x1, Pallas kernels: 78.9 us -> 75.4 us  [shards(): pl.pallas_call(functools.partial(kernel, nt, nf, nc, hl), out_shape=(V((L...]
where the time goes in v3:
time: 77.2 us; the launch traced here: 77 us
  Pallas kernels  76.4 us (99%)
    pallas_call x1, Pallas kernels, shards(): pl.pallas_call(functools.partial(kernel, nt, nf, nc, hl), out_shape=(V((L...  75.4 us

profile of v3, /device:TPU:0, one launch (start us, length us, event | category | flops | bytes accessed | tf_op | source)
XLA Modules:
  0.0 77.0 jit_solution(11560441188543831089)
XLA Ops:
  0.6 75.4 %shard_map.157 = (bf16[128,2560]{1,0:T(8,128)(2,1)S(1)}, f32[16,1280]{1,0:T(8,128)S(1)}, f32[16,2560]{1,0:T(8,128)S(1)}) custom-call(bf16[128,5120]{1,0:T(8,128)(2,1)} %bitcast.13, bf16[128,256]{1,0:T(8,128)(2,1)} %bitcast.16, bf16[128,5120]{1,0:T(8,128)(2,1)} %bitcast.14, bf16[80,128]{1,0:T(8,128)(2,1)} %bitcast.18, f32[4,5376]{1,0:T(4,128)} %taps_hbm.1, ...), custom_call_target="tpu_custom_call" | custom-call | tf_op jit(solution)/shard_map/pallas_call | solution.py:661
  76.1 0.9 %shard_map.158 = (bf16[128,2560]{1,0:T(8,128)(2,1)}, f32[16,1280]{1,0:T(8,128)}, f32[16,2560]{1,0:T(8,128)}) custom-call(bf16[128,2560]{1,0:T(8,128)(2,1)S(1)} %get-tuple-element.9.mixed, f32[16,1280]{1,0:T(8,128)S(1)} %get-tuple-element.10.ga, f32[16,2560]{1,0:T(8,128)S(1)} %get-tuple-element.11.gb), custom_call_target="tpu_custom_call" | custom-call | tf_op jit(solution)/shard_map/pallas_call | solution.py:672

commit v4 on v3

--- a/solution.py
+++ b/solution.py
@@ -38,9 +38,8 @@
 
 
 def column_chunks(width):
-    lanes = width // 128
-    first = -(-lanes // 2)
-    return [(0, first * 128), (first * 128, (lanes - first) * 128)] if lanes > 1 else [(0, width)]
+    first = max(width - 128, 128)
+    return [(0, first), (first, width - first)] if width > first else [(0, width)]
 
 
 def kernel(
@@ -117,20 +116,17 @@
     nxt, prv = lax.rem(idx + 1, total), lax.rem(idx + total - 1, total)
     bar = pltpu.get_barrier_semaphore()
     greet = [{"tensor": pt[e]} for e in range(1, nt)]
-    greet += [{"fsdp": lax.rem(f + d, nf)} for d in range(1, nf)]
     greet += [{"context": lax.rem(c + k, nc)} for k in range(1, nc)]
     greet += [place(nxt), place(prv)]
     for dev in greet:
         pl.semaphore_signal(bar, inc=1, device_id=dev, device_id_type=MESH)
-    for cp in loads:
-        cp.wait()
-    dt_all[t] = dt_ref[...]
-    pl.semaphore_wait(bar, len(greet))
-
-    h1 = copy(x_ref.at[L - HALO : L, :], halo_x, h_ss.at[0], h_rs.at[0], place(nxt))
-    h2 = copy(bc_ref.at[L - HALO : L, :], halo_bc, h_ss.at[1], h_rs.at[1], place(nxt))
-    for e in range(1, nt):
-        copy(dt_ref, dt_all.at[t], dt_ss.at[0], dt_rs.at[0], {"tensor": pt[e]})
+    for near, to in ((f >= 1, f - 1), (f + 1 < nf, f + 1)):
+        @pl.when(near)
+        def _(to=to):
+            pl.semaphore_signal(bar, inc=1, device_id={"fsdp": to}, device_id_type=MESH)
+
+    pl.semaphore_wait(bar, len(greet) + (f >= 1).astype(jnp.int32) + (f + 1 < nf).astype(jnp.int32))
+
     share = pl.ds(pl.multiple_of(c * R, 16), R)
 
     def w_copy(dr, s, ch, q):
@@ -160,6 +156,14 @@
             @pl.when(sends(dr, 0))
             def _(dr=dr, ch=ch):
                 w_copy(dr, 0, ch, f).start()
+
+    for cp in loads:
+        cp.wait()
+    h1 = copy(x_ref.at[L - HALO : L, :], halo_x, h_ss.at[0], h_rs.at[0], place(nxt))
+    h2 = copy(bc_ref.at[L - HALO : L, :], halo_bc, h_ss.at[1], h_rs.at[1], place(nxt))
+    for e in range(1, nt):
+        copy(dt_ref, dt_all.at[t], dt_ss.at[0], dt_rs.at[0], {"tensor": pt[e]})
+    dt_all[t] = dt_ref[...]
 
     def w_arrive(s, ch):
         for dr in range(2):
@@ -317,13 +321,20 @@
         stl[b, 0:N, :] = state
         state = loc_s[b, N : N + 1, :] * state + loc_s[b, 0:N, :]
     msg[0:N, :] = state.astype(BF)
-    sts = [
-        copy(msg, st_in.at[c], st_ss.at[k], st_rs.at[k], {"context": lax.rem(c + k, nc)})
-        for k in range(1, nc)
-    ]
-
-    for cp in sts:
-        cp.wait()
+
+    def state_copy(k, src):
+        return remote(msg, st_in.at[src], st_ss.at[k], st_rs.at[k], {"context": lax.rem(c + k, nc)})
+
+    for k in range(1, nc):
+        @pl.when(c + k < nc)
+        def _(k=k):
+            state_copy(k, c).start()
+
+    for k in range(1, nc):
+        @pl.when(c >= k)
+        def _(k=k):
+            state_copy(k, lax.rem(c + nc - k, nc)).wait_recv()
+
     inc_s[...] = jnp.zeros_like(inc_s)
 
     def chain(k, carry):
@@ -396,8 +407,6 @@
     units = [(0, None, 0, W)] + [(s, ch) + chunks[ch] for s in range(1, nf) for ch in range(len(chunks))]
     spans = [pl.ds(pl.multiple_of(order[s] * W + off, 128), wide) for s, _, off, wide in units]
 
-    held = max(nt - 1, 1)
-
     def gate(e, carry):
         b = peer(e)
         rows = pl.ds(pl.multiple_of(b * L, L), L)
@@ -435,7 +444,7 @@
         by, bx = lax.div(b, nx), lax.rem(b, nx)
         rs_send[by, bx, :, spans[0]] = dot(out, wbuf[f]).astype(BF)
 
-        @pl.when((e > 0) & (e < held))
+        @pl.when(e > 0)
         def _():
             send_block(0, by, bx)
 
@@ -459,6 +468,7 @@
     nch = len(chunks)
     for ch in range(nch):
         project(1 + ch)
+        send_unit(1 + ch)
     landed(ad_in.at[1:nt], ad_rs.at[0])
     red = adx[t]
     for e in range(1, nt):
@@ -477,10 +487,6 @@
             gb_own.at[:, pl.ds(pl.multiple_of(pt[e] * part, 128), part)],
             gb_in.at[e], ga_ss.at[0], ga_rs.at[0], {"tensor": pt[e]},
         )
-    for e in range(held, nt):
-        send_block(0, lax.div(pt[e], nx), lax.rem(pt[e], nx))
-    for ch in range(nch):
-        send_unit(1 + ch)
     scale_col = dot(jnp.broadcast_to(scale_row, (8, L)), jnp.full((8, 128), 0.125, F32), 0, 0, HI)[:, 0:1]
     if steps > 1:
         for ch in range(1, nch):
@@ -493,38 +499,10 @@
             project(1 + (s - 1) * nch + ch)
             send_unit(1 + (s - 1) * nch + ch)
     second(0)
+    for ch in range(nch):
+        second(1 + ch)
     landed(ag_all.at[0 : nt - 1], ag_rs.at[0])
     landed(gb_in.at[1:nt], ga_rs.at[0])
-    ag_all[t] = ag_own[...]
-    grad = jnp.zeros((16, LW), F32)
-    for s in range(nt):
-        grad = grad + dot(ag_all[s], g_s[s * L : (s + 1) * L, :])
-    comb[:, 0:LW] = grad
-    acc = gb_own[:, own_part].astype(F32)
-    for e in range(1, nt):
-        acc = acc + gb_in[e].astype(F32)
-    comb[:, LW : LW + part] = acc
-    lanes = (LW + part) // 128
-    per = -(-lanes // nc)
-
-    def seg(i):
-        return pl.ds(pl.multiple_of(jnp.minimum(i * per, lanes - per) * 128, 128), per * 128)
-
-    ccs = [
-        copy(comb.at[:, seg(lax.rem(c + k, nc))], comb_c.at[k], cc_ss.at[k], cc_rs.at[k], {"context": lax.rem(c + k, nc)})
-        for k in range(1, nc)
-    ]
-    for ch in range(nch):
-        second(1 + ch)
-    for cp in ccs:
-        cp.wait()
-    acc = comb[:, seg(c)]
-    for k in range(1, nc):
-        acc = acc + comb_c[k]
-    comb2[...] = acc.astype(BF)
-    for k in range(1, nf):
-        copy(comb2, comb_f.at[f], cf_ss.at[0], cf_rs.at[0], {"fsdp": lax.rem(f + k, nf)})
-    comb_f[f] = comb2[...]
     def finish(u):
         cols = spans[u]
         up_part = rs_send[yi, xi, top, cols].astype(F32)
@@ -541,22 +519,55 @@
         acc = jnp.concatenate([up_part, low_part], axis=0) + 2.0 * dot(ad16, up_ref[:, cols], 0, 0)
         mixed_ref[:, cols] = (scale_col * acc).astype(BF)
 
+    ag_all[t] = ag_own[...]
+    grad = jnp.zeros((16, LW), F32)
+    for s in range(nt):
+        grad = grad + dot(ag_all[s], g_s[s * L : (s + 1) * L, :])
+    comb[:, 0:LW] = grad
+    acc = gb_own[:, own_part].astype(F32)
+    for e in range(1, nt):
+        acc = acc + gb_in[e].astype(F32)
+    comb[:, LW : LW + part] = acc
+    lanes = (LW + part) // 128
+    per = -(-lanes // nc)
+
+    def seg(i):
+        return pl.ds(pl.multiple_of(jnp.minimum(i * per, lanes - per) * 128, 128), per * 128)
+
+    ccs = [
+        copy(comb.at[:, seg(lax.rem(c + k, nc))], comb_c.at[k], cc_ss.at[k], cc_rs.at[k], {"context": lax.rem(c + k, nc)})
+        for k in range(1, nc)
+    ]
     finish(0)
+    for cp in ccs:
+        cp.wait()
+    acc = comb[:, seg(c)]
+    for k in range(1, nc):
+        acc = acc + comb_c[k]
+    comb2[...] = acc.astype(BF)
+    comb_f[f] = comb2[...]
     for u in range(1 + nch, 1 + (nf - 2) * nch):
         second(u)
     for ch in range(nch):
         finish(1 + ch)
     last = 1 + (nf - 2) * nch
     for ch in range(nch):
+
         if steps > 2:
             w_arrive(steps - 1, ch)
+        if ch == 0:
+            for k in range(1, nf):
+                copy(comb2, comb_f.at[f], cf_ss.at[0], cf_rs.at[0], {"fsdp": lax.rem(f + k, nf)})
         if nf > 2:
+
             project(last + ch)
             send_unit(last + ch)
         if ch == 0:
+
             for u in range(1 + nch, last):
                 finish(u)
     if nf > 2:
+
         for ch in range(nch - 1):
             second(last + ch)
     landed(comb_f.at[0 : nf - 1], cf_rs.at[0])
@@ -583,6 +594,11 @@
     for s in range(nt):
         gb_ref[:, s * part : (s + 1) * part] = fin[s]
     sent(dt_all.at[0 : nt - 1], dt_ss.at[0])
+    for k in range(1, nc):
+        @pl.when(c + k < nc)
+        def _(k=k):
+            state_copy(k, c).wait_send()
+
     sent(bc_all.at[0 : (nt - 1) * L, :], bc_ss.at[0])
     sent(z_all.at[0 : (nt - 1) * L, :], z_ss.at[0])
     sent(ad_in.at[1:nt], ad_ss.at[0])

time: 77.2 us -> 73 us (0.946)
  Pallas kernels: 76.4 us -> 72.2 us
    pallas_call x1, Pallas kernels: 75.4 us -> 71.2 us  [shards(): pl.pallas_call(functools.partial(kernel, nt, nf, nc, hl), out_shape=(V((L...]
where the time goes in v4:
time: 73 us; the launch traced here: 72.8 us
  Pallas kernels  72.2 us (99%)
    pallas_call x1, Pallas kernels, shards(): pl.pallas_call(functools.partial(kernel, nt, nf, nc, hl), out_shape=(V((L...  71.2 us

profile of v4, /device:TPU:0, one launch (start us, length us, event | category | flops | bytes accessed | tf_op | source)
XLA Modules:
  0.0 72.8 jit_solution(10547130668618117018)
XLA Ops:
  0.6 71.2 %shard_map.157 = (bf16[128,2560]{1,0:T(8,128)(2,1)S(1)}, f32[16,1280]{1,0:T(8,128)S(1)}, f32[16,2560]{1,0:T(8,128)S(1)}) custom-call(bf16[128,5120]{1,0:T(8,128)(2,1)} %bitcast.13, bf16[128,256]{1,0:T(8,128)(2,1)} %bitcast.16, bf16[128,5120]{1,0:T(8,128)(2,1)} %bitcast.14, bf16[80,128]{1,0:T(8,128)(2,1)} %bitcast.18, f32[4,5376]{1,0:T(4,128)} %taps_hbm.1, ...), custom_call_target="tpu_custom_call" | custom-call | tf_op jit(solution)/shard_map/pallas_call | solution.py:677
  71.9 0.9 %shard_map.158 = (bf16[128,2560]{1,0:T(8,128)(2,1)}, f32[16,1280]{1,0:T(8,128)}, f32[16,2560]{1,0:T(8,128)}) custom-call(bf16[128,2560]{1,0:T(8,128)(2,1)S(1)} %get-tuple-element.9.mixed, f32[16,1280]{1,0:T(8,128)S(1)} %get-tuple-element.10.ga, f32[16,2560]{1,0:T(8,128)S(1)} %get-tuple-element.11.gb), custom_call_target="tpu_custom_call" | custom-call | tf_op jit(solution)/shard_map/pallas_call | solution.py:688

commit v5 on v4

--- a/solution.py
+++ b/solution.py
@@ -34,12 +34,13 @@
 
 
 def grid_of(count):
-    return (2, count // 2) if count % 2 == 0 else (1, count)
+    return 2, count // 2
 
 
 def column_chunks(width):
-    first = max(width - 128, 128)
-    return [(0, first), (first, width - first)] if width > first else [(0, width)]
+    first = max(width // 256 * 128, 128)
+    cuts = sorted({0, min(first, width), min(max(width - 128, first), width), width})
+    return [(a, b - a) for a, b in zip(cuts, cuts[1:])]
 
 
 def kernel(
@@ -49,7 +50,7 @@
     x_ref, bc_ref, dt_ref, taps_ref, bias_ref, gain_ref, down_ref, up_ref, cot_ref,
     halo_x, halo_bc, x_send, x_all, z_all, bc_all, dt_all, wbuf, a_s, step_s, at_s, stept_s,
     stl, loc_s, skip_s, msg, st_in, inc_s, e_s, y_s, g_s, adx, ad_in, ag_own, ag_all, gb_own, gb_in,
-    comb, comb_c, comb2, comb_f, seg_own, seg_in, full, fin, rs_send, rs_xa, rs_yb, sum_a, in_a, sum_b, in_b,
+    comb, comb_c, comb2, comb_f, seg_own, seg_in, full, fin, rs_send, rs_in, sums, sums_in, rs_near,
     ld, h_ss, h_rs, dt_ss, dt_rs, bc_ss, bc_rs, x_ss, x_rs, z_ss, z_rs, w_ss, w_rs, wf_ss, wf_rs, st_ss, st_rs,
     ad_ss, ad_rs, ag_ss, ag_rs, ga_ss, ga_rs, cc_ss, cc_rs, cf_ss, cf_rs, sg_ss, sg_rs, fin_ss, fin_rs, rs_ss, rs_rs, loc,
 ):
@@ -66,6 +67,7 @@
     total = nc * nt
     bits = [1 << i for i in range(nt.bit_length() - 1)]
     chunks = column_chunks(W)
+    nch = len(chunks)
     steps = nf - 1
 
     def peer(e):
@@ -330,6 +332,8 @@
         def _(k=k):
             state_copy(k, c).start()
 
+    if steps > 1:
+        w_arrive(1, 0)
     for k in range(1, nc):
         @pl.when(c >= k)
         def _(k=k):
@@ -351,61 +355,64 @@
     top, low = slice(0, L // 2), slice(L // 2, L)
     xo = nx - 1 - xi
 
-    def to_x(u, by):
+    def to_x(u, by, count):
         return remote(
-            rs_send.at[by, xo, top, spans[u]], rs_xa.at[by, :, spans[u]], rs_ss.at[0], rs_rs.at[u, 0],
-            {"tensor": yi * nx + xo},
+            rs_send.at[pl.ds(by, count), xo, top, spans[u]], rs_in.at[pl.ds(by, count), :, spans[u]],
+            rs_ss.at[0], rs_rs.at[u, 0], {"tensor": yi * nx + xo},
         )
 
-    def to_y(u, j, bx):
+    def to_y(u, j, bx, count):
         ty = lax.rem(yi + j, ny)
-        return remote(
-            rs_send.at[ty, bx, low, spans[u]], rs_yb.at[ny - j - 1, bx, :, spans[u]], rs_ss.at[1], rs_rs.at[u, 1],
-            {"tensor": ty * nx + xi},
-        )
+        src = rs_send.at[ty, pl.ds(bx, count), low, spans[u]]
+        dst = rs_in.at[pl.ds(ny + (ny - j - 1) * nx + bx, count), :, spans[u]]
+        return remote(src, dst, rs_ss.at[0], rs_rs.at[u, 0], {"tensor": ty * nx + xi})
 
     def send_block(u, by, bx):
         @pl.when(bx != xi)
         def _():
-            to_x(u, by).start()
+            to_x(u, by, 1).start()
 
         for j in range(1, ny):
             @pl.when(lax.rem(yi + j, ny) == by)
             def _(j=j):
-                to_y(u, j, bx).start()
+                to_y(u, j, bx, 1).start()
 
     def send_unit(u):
-        if nx > 1:
-            to_x(u, slice(None)).start()
+        if u == len(units) - 1:
+            for e in range(1, nt):
+                remote(
+                    rs_send.at[lax.div(pt[e], nx), lax.rem(pt[e], nx), :, spans[u]], rs_near.at[e - 1],
+                    rs_ss.at[2], rs_rs.at[u, 0], {"tensor": pt[e]},
+                ).start()
+            return
+        to_x(u, 0, ny).start()
         for j in range(1, ny):
-            to_y(u, j, slice(None)).start()
+            to_y(u, j, 0, nx).start()
+
+    def from_y(j, bx, cols):
+        return rs_in[ny + (j - 1) * nx + bx, :, cols].astype(F32)
 
     def second(u):
         cols = spans[u]
-        if nx > 1:
-            landed(rs_xa.at[:, :, cols], rs_rs.at[u, 0])
-        if ny > 1:
-            landed(rs_yb.at[:, :, :, cols], rs_rs.at[u, 1])
+        landed(rs_in.at[:, :, cols], rs_rs.at[u, 0])
         for j in range(1, ny):
             ty = lax.rem(yi + j, ny)
-            acc = rs_send[ty, xi, top, cols].astype(F32)
-            if nx > 1:
-                acc = acc + rs_xa[ty, :, cols].astype(F32)
-            sum_a[j - 1, :, cols] = acc.astype(BF)
+            sums[j - 1, :, cols] = (rs_send[ty, xi, top, cols].astype(F32) + rs_in[ty, :, cols].astype(F32)).astype(BF)
             remote(
-                sum_a.at[j - 1, :, cols], in_a.at[ny - j - 1, :, cols], rs_ss.at[2], rs_rs.at[u, 2], {"tensor": ty * nx + xi}
+                sums.at[j - 1, :, cols], sums_in.at[ny - j - 1, :, cols], rs_ss.at[1], rs_rs.at[u, 1],
+                {"tensor": ty * nx + xi},
             ).start()
-        if nx > 1:
-            acc = rs_send[yi, xo, low, cols].astype(F32)
-            for j in range(1, ny):
-                acc = acc + rs_yb[j - 1, xo, :, cols].astype(F32)
-            sum_b[:, cols] = acc.astype(BF)
-            remote(
-                sum_b.at[:, cols], in_b.at[:, cols], rs_ss.at[3], rs_rs.at[u, 3], {"tensor": yi * nx + xo}
-            ).start()
-
-    units = [(0, None, 0, W)] + [(s, ch) + chunks[ch] for s in range(1, nf) for ch in range(len(chunks))]
-    spans = [pl.ds(pl.multiple_of(order[s] * W + off, 128), wide) for s, _, off, wide in units]
+        acc = rs_send[yi, xo, low, cols].astype(F32)
+        for j in range(1, ny):
+            acc = acc + from_y(j, xo, cols)
+        sums[ny - 1, :, cols] = acc.astype(BF)
+        remote(
+            sums.at[ny - 1, :, cols], sums_in.at[ny - 1, :, cols], rs_ss.at[1], rs_rs.at[u, 1],
+            {"tensor": yi * nx + xo},
+        ).start()
+
+    units = [(s, 0, W) for s in range(nf - 1)] + [(nf - 1,) + chunk for chunk in chunks]
+    spans = [pl.ds(pl.multiple_of(order[s] * W + off, 128), wide) for s, off, wide in units]
 
     def gate(e, carry):
         b = peer(e)
@@ -418,7 +425,8 @@
         if steps > 1:
             @pl.when(e == nt - 1)
             def _():
-                w_arrive(1, 0)
+                for ch in range(1, nch - 1):
+                    w_arrive(1, ch)
 
         @pl.when(e > 0)
         def _():
@@ -453,8 +461,10 @@
     lax.fori_loop(0, nt, gate, 0)
 
     def project(u):
-        slot, ch, off, wide = units[u]
-        w_ready(slot, ch)
+        slot, off, wide = units[u]
+        for ch in range(nch):
+            if off <= chunks[ch][0] < off + wide:
+                w_ready(slot, ch)
 
         def lap(by, carry):
             rows = pl.ds(pl.multiple_of(by * (nx * L), L), nx * L)
@@ -465,10 +475,11 @@
 
         lax.fori_loop(0, ny, lap, 0)
 
-    nch = len(chunks)
-    for ch in range(nch):
-        project(1 + ch)
-        send_unit(1 + ch)
+    project(1)
+    send_unit(1)
+    if steps > 1:
+        for ch in range(max(nch - 1, 1), nch):
+            w_arrive(1, ch)
     landed(ad_in.at[1:nt], ad_rs.at[0])
     red = adx[t]
     for e in range(1, nt):
@@ -488,35 +499,32 @@
             gb_in.at[e], ga_ss.at[0], ga_rs.at[0], {"tensor": pt[e]},
         )
     scale_col = dot(jnp.broadcast_to(scale_row, (8, L)), jnp.full((8, 128), 0.125, F32), 0, 0, HI)[:, 0:1]
-    if steps > 1:
-        for ch in range(1, nch):
-            w_arrive(1, ch)
     for s in range(2, nf - 1):
         if s > 2:
             for ch in range(nch):
                 w_arrive(s - 1, ch)
-        for ch in range(nch):
-            project(1 + (s - 1) * nch + ch)
-            send_unit(1 + (s - 1) * nch + ch)
+        project(s)
+        send_unit(s)
     second(0)
-    for ch in range(nch):
-        second(1 + ch)
+    second(1)
     landed(ag_all.at[0 : nt - 1], ag_rs.at[0])
     landed(gb_in.at[1:nt], ga_rs.at[0])
     def finish(u):
         cols = spans[u]
-        up_part = rs_send[yi, xi, top, cols].astype(F32)
-        low_part = rs_send[yi, xi, low, cols].astype(F32)
-        if nx > 1:
-            landed(in_b.at[:, cols], rs_rs.at[u, 3])
-            up_part = up_part + rs_xa[yi, :, cols].astype(F32)
-            low_part = low_part + in_b[:, cols].astype(F32)
-        if ny > 1:
-            landed(in_a.at[:, :, cols], rs_rs.at[u, 2])
-        for j in range(1, ny):
-            up_part = up_part + in_a[j - 1, :, cols].astype(F32)
-            low_part = low_part + rs_yb[j - 1, xi, :, cols].astype(F32)
-        acc = jnp.concatenate([up_part, low_part], axis=0) + 2.0 * dot(ad16, up_ref[:, cols], 0, 0)
+        if u == len(units) - 1:
+            landed(rs_near, rs_rs.at[u, 0])
+            acc = rs_send[yi, xi, :, cols].astype(F32)
+            for e in range(1, nt):
+                acc = acc + rs_near[e - 1].astype(F32)
+        else:
+            landed(sums_in.at[:, :, cols], rs_rs.at[u, 1])
+            up_part = rs_send[yi, xi, top, cols].astype(F32) + rs_in[yi, :, cols].astype(F32)
+            low_part = rs_send[yi, xi, low, cols].astype(F32) + sums_in[ny - 1, :, cols].astype(F32)
+            for j in range(1, ny):
+                up_part = up_part + sums_in[j - 1, :, cols].astype(F32)
+                low_part = low_part + from_y(j, xi, cols)
+            acc = jnp.concatenate([up_part, low_part], axis=0)
+        acc = acc + 2.0 * dot(ad16, up_ref[:, cols], 0, 0)
         mixed_ref[:, cols] = (scale_col * acc).astype(BF)
 
     ag_all[t] = ag_own[...]
@@ -538,6 +546,26 @@
         copy(comb.at[:, seg(lax.rem(c + k, nc))], comb_c.at[k], cc_ss.at[k], cc_rs.at[k], {"context": lax.rem(c + k, nc)})
         for k in range(1, nc)
     ]
+    last = nf - 1
+    for u in range(2, last):
+        second(u)
+    near = dist[nf - 1] < steps - 1
+
+    def last_slot(ch):
+        project(last + ch)
+        send_unit(last + ch)
+
+    @pl.when(near)
+    def _():
+        for ch in range(nch):
+            last_slot(ch)
+
+    w_arrive(steps - 1, 0)
+
+    @pl.when(jnp.logical_not(near))
+    def _():
+        last_slot(0)
+
     finish(0)
     for cp in ccs:
         cp.wait()
@@ -546,30 +574,20 @@
         acc = acc + comb_c[k]
     comb2[...] = acc.astype(BF)
     comb_f[f] = comb2[...]
-    for u in range(1 + nch, 1 + (nf - 2) * nch):
-        second(u)
-    for ch in range(nch):
-        finish(1 + ch)
-    last = 1 + (nf - 2) * nch
-    for ch in range(nch):
-
-        if steps > 2:
-            w_arrive(steps - 1, ch)
-        if ch == 0:
-            for k in range(1, nf):
-                copy(comb2, comb_f.at[f], cf_ss.at[0], cf_rs.at[0], {"fsdp": lax.rem(f + k, nf)})
-        if nf > 2:
-
-            project(last + ch)
-            send_unit(last + ch)
-        if ch == 0:
-
-            for u in range(1 + nch, last):
+    finish(1)
+    for k in range(1, nf):
+        copy(comb2, comb_f.at[f], cf_ss.at[0], cf_rs.at[0], {"fsdp": lax.rem(f + k, nf)})
+    for ch in range(1, nch):
+        w_arrive(steps - 1, ch)
+
+        @pl.when(jnp.logical_not(near))
+        def _(ch=ch):
+            last_slot(ch)
+
+        if ch == 1:
+            for u in range(2, last):
                 finish(u)
-    if nf > 2:
-
-        for ch in range(nch - 1):
-            second(last + ch)
+            second(last)
     landed(comb_f.at[0 : nf - 1], cf_rs.at[0])
     acc = comb_f[0].astype(F32)
     for k in range(1, nf):
@@ -577,22 +595,21 @@
     seg_own[...] = acc
     sgs = [copy(seg_own, seg_in.at[c], sg_ss.at[k], sg_rs.at[k], {"context": lax.rem(c + k, nc)}) for k in range(1, nc)]
     seg_in[c] = acc
-    if nf > 2:
-        second(last + nch - 1)
+    for ch in range(1, nch - 1):
+        second(last + ch)
     for cp in sgs:
         cp.wait()
     for i in range(nc):
         full[:, seg(i)] = seg_in[i]
     ga_ref[...] = full[:, 0:LW]
-    fin[t] = full[:, LW : LW + part]
+    fin[t] = full[:, LW : LW + part].astype(BF)
     for e in range(1, nt):
         copy(fin.at[t], fin.at[t], fin_ss.at[0], fin_rs.at[0], {"tensor": pt[e]})
-    if nf > 2:
-        for ch in range(nch):
-            finish(last + ch)
+    for ch in range(nch):
+        finish(last + ch)
     landed(fin.at[0 : nt - 1], fin_rs.at[0])
     for s in range(nt):
-        gb_ref[:, s * part : (s + 1) * part] = fin[s]
+        gb_ref[:, s * part : (s + 1) * part] = fin[s].astype(F32)
     sent(dt_all.at[0 : nt - 1], dt_ss.at[0])
     for k in range(1, nc):
         @pl.when(c + k < nc)
@@ -606,12 +623,10 @@
     sent(gb_in.at[1:nt], ga_ss.at[0])
     sent(comb_f.at[0 : nf - 1], cf_ss.at[0])
     sent(fin.at[0 : nt - 1], fin_ss.at[0])
-    if nx > 1:
-        sent(rs_xa, rs_ss.at[0])
-        sent(in_b, rs_ss.at[3])
-    if ny > 1:
-        sent(rs_yb, rs_ss.at[1])
-        sent(in_a, rs_ss.at[2])
+    head = slice(0, rs_in.shape[2] - chunks[-1][1])
+    sent(rs_in.at[:, :, head], rs_ss.at[0])
+    sent(sums_in.at[:, :, head], rs_ss.at[1])
+    sent(rs_near, rs_ss.at[2])
     for s in range(steps):
         for dr in range(2):
             @pl.when(sends(dr, s))
@@ -645,11 +660,10 @@
     T = nt * L
     part = M // nt
     nx, ny = grid_of(nt)
-    my = max(ny - 1, 1)
     dt = dt[0].T
     down = down.T
     nch = len(column_chunks(W))
-    units = 1 + (nf - 1) * nch
+    units = nf - 1 + nch
     lanes = (LW + part) // 128
     SW = -(-lanes // nc) * 128
     vm = pl.BlockSpec(memory_space=pltpu.VMEM)
@@ -667,12 +681,12 @@
         V((16, L), BF), V((nt, 16, L), BF), V((16, M), BF), V((nt, 16, part), BF),
         V((16, LW + part), F32), V((nc, 16, SW), F32), V((16, SW), BF), V((nf, 16, SW), BF),
         V((16, SW), F32), V((nc, 16, SW), F32), V((16, LW + part), F32),
-        V((nt, 16, part), F32), V((ny, nx, L, M), BF), V((ny, L // 2, M), BF), V((my, nx, L // 2, M), BF),
-        V((my, L // 2, M), BF), V((my, L // 2, M), BF), V((L // 2, M), BF), V((L // 2, M), BF),
+        V((nt, 16, part), BF), V((ny, nx, L, M), BF), V((ny + (ny - 1) * nx, L // 2, M), BF),
+        V((ny, L // 2, M), BF), V((ny, L // 2, M), BF), V((nt - 1, L, column_chunks(W)[-1][1]), BF),
         D((9,)), D((2,)), D((2,)), D((1,)), D((1,)), D((1,)), D((nt,)), D((1,)), D((nt,)), D((1,)), D((nt,)),
         D((2, nf - 1)), D((2, nf - 1, nch)), D((2, nf - 1)), D((2, nf - 1, nch)), D((nc,)), D((nc,)),
         D((1,)), D((1,)), D((1,)), D((1,)), D((1,)), D((1,)), D((nc,)), D((nc,)), D((1,)), D((1,)),
-        D((nc,)), D((nc,)), D((1,)), D((1,)), D((4,)), D((units, 4)), D((2,)),
+        D((nc,)), D((nc,)), D((1,)), D((1,)), D((3,)), D((units, 2)), D((2,)),
     ]
     mixed, ga, gb = pl.pallas_call(
         functools.partial(kernel, nt, nf, nc, hl),

time: 73 us -> 70.4 us (0.964)
  Pallas kernels: 72.2 us -> 69.6 us
    pallas_call x1, Pallas kernels: 71.2 us -> 68.7 us  [shards(): pl.pallas_call(functools.partial(kernel, nt, nf, nc, hl), out_shape=(V((L...]
where the time goes in v5:
time: 70.4 us; the launch traced here: 70.2 us
  Pallas kernels  69.6 us (99%)
    pallas_call x1, Pallas kernels, shards(): pl.pallas_call(functools.partial(kernel, nt, nf, nc, hl), out_shape=(V((L...  68.7 us

profile of v5, /device:TPU:0, one launch (start us, length us, event | category | flops | bytes accessed | tf_op | source)
XLA Modules:
  0.0 70.2 jit_solution(10437590814279030126)
XLA Ops:
  0.6 68.7 %shard_map.157 = (bf16[128,2560]{1,0:T(8,128)(2,1)S(1)}, f32[16,1280]{1,0:T(8,128)S(1)}, f32[16,2560]{1,0:T(8,128)S(1)}) custom-call(bf16[128,5120]{1,0:T(8,128)(2,1)} %bitcast.13, bf16[128,256]{1,0:T(8,128)(2,1)} %bitcast.16, bf16[128,5120]{1,0:T(8,128)(2,1)} %bitcast.14, bf16[80,128]{1,0:T(8,128)(2,1)} %bitcast.18, f32[4,5376]{1,0:T(4,128)} %taps_hbm.1, ...), custom_call_target="tpu_custom_call" | custom-call | tf_op jit(solution)/shard_map/pallas_call | solution.py:691
  69.3 0.9 %shard_map.158 = (bf16[128,2560]{1,0:T(8,128)(2,1)}, f32[16,1280]{1,0:T(8,128)}, f32[16,2560]{1,0:T(8,128)}) custom-call(bf16[128,2560]{1,0:T(8,128)(2,1)S(1)} %get-tuple-element.9.mixed, f32[16,1280]{1,0:T(8,128)S(1)} %get-tuple-element.10.ga, f32[16,2560]{1,0:T(8,128)S(1)} %get-tuple-element.11.gb), custom_call_target="tpu_custom_call" | custom-call | tf_op jit(solution)/shard_map/pallas_call | solution.py:702

commit v6 on v5

--- a/solution.py
+++ b/solution.py
@@ -38,21 +38,20 @@
 
 
 def column_chunks(width):
-    first = max(width // 256 * 128, 128)
-    cuts = sorted({0, min(first, width), min(max(width - 128, first), width), width})
+    cuts = sorted({0, max(width - 256, 128), max(width - 128, 128), width})
     return [(a, b - a) for a, b in zip(cuts, cuts[1:])]
 
 
 def kernel(
     nt, nf, nc, hl,
-    x_hbm, bc_hbm, z_ref, dt_hbm, taps_hbm, bias_hbm, sb_ref, dr_ref, sk_ref, gain_hbm, w_ref, down_hbm, up_hbm, cot_hbm,
+    x_hbm, bc_hbm, z_ref, dt_hbm, taps_hbm, bias_hbm, sb_hbm, dr_hbm, sk_hbm, gain_hbm, w_ref, down_hbm, up_hbm, cot_hbm,
     mixed_ref, ga_ref, gb_ref,
-    x_ref, bc_ref, dt_ref, taps_ref, bias_ref, gain_ref, down_ref, up_ref, cot_ref,
+    x_ref, bc_ref, dt_ref, taps_ref, bias_ref, gain_ref, down_ref, up_ref, cot_ref, sb_ref, dr_ref, sk_ref,
     halo_x, halo_bc, x_send, x_all, z_all, bc_all, dt_all, wbuf, a_s, step_s, at_s, stept_s,
     stl, loc_s, skip_s, msg, st_in, inc_s, e_s, y_s, g_s, adx, ad_in, ag_own, ag_all, gb_own, gb_in,
-    comb, comb_c, comb2, comb_f, seg_own, seg_in, full, fin, rs_send, rs_in, sums, sums_in, rs_near,
+    comb, comb_c, comb2, comb_f, tot, seg_in, full, fin, rs_send, rs_in, sums, sums_in, rs_near,
     ld, h_ss, h_rs, dt_ss, dt_rs, bc_ss, bc_rs, x_ss, x_rs, z_ss, z_rs, w_ss, w_rs, wf_ss, wf_rs, st_ss, st_rs,
-    ad_ss, ad_rs, ag_ss, ag_rs, ga_ss, ga_rs, cc_ss, cc_rs, cf_ss, cf_rs, sg_ss, sg_rs, fin_ss, fin_rs, rs_ss, rs_rs, loc,
+    ad_ss, ad_rs, ag_ss, ag_rs, ga_ss, ga_rs, cc_ss, cc_rs, cf_ss, cf_rs, tot_ss, tot_rs, sg_ss, sg_rs, fin_ss, fin_rs, rs_ss, rs_rs, loc,
 ):
     t = lax.axis_index("tensor")
     f = lax.axis_index("fsdp")
@@ -100,16 +99,17 @@
         cp.start()
         return cp
 
+    own_w = pltpu.make_async_copy(w_ref, wbuf.at[f], loc.at[0])
+    own_w.start()
     loads = []
     for i, (src, dst) in enumerate((
         (x_hbm, x_ref), (bc_hbm, bc_ref), (dt_hbm, dt_ref), (taps_hbm, taps_ref), (bias_hbm, bias_ref),
         (gain_hbm, gain_ref), (down_hbm, down_ref), (up_hbm, up_ref), (cot_hbm, cot_ref),
+        (sb_hbm, sb_ref), (dr_hbm, dr_ref), (sk_hbm, sk_ref),
     )):
         cp = pltpu.make_async_copy(src, dst, ld.at[i])
         cp.start()
         loads.append(cp)
-    own_w = pltpu.make_async_copy(w_ref, wbuf.at[f], loc.at[0])
-    own_w.start()
     own_rows = pl.ds(pl.multiple_of(t * L, L), L)
     own_cols = pl.ds(pl.multiple_of(t * LW, 128), LW)
     own_z = pltpu.make_async_copy(z_ref.at[:, own_cols], z_all.at[own_rows, :], loc.at[1])
@@ -129,17 +129,18 @@
 
     pl.semaphore_wait(bar, len(greet) + (f >= 1).astype(jnp.int32) + (f + 1 < nf).astype(jnp.int32))
 
+    own_w.wait()
     share = pl.ds(pl.multiple_of(c * R, 16), R)
 
     def w_copy(dr, s, ch, q):
         cols = pl.ds(chunks[ch][0], chunks[ch][1])
-        src = w_ref.at[share, cols] if s == 0 else wbuf.at[q, share, cols]
+        src = wbuf.at[q, share, cols]
         to = f + 1 if dr == 0 else f - 1
-        return remote(src, wbuf.at[q, share, cols], w_ss.at[dr, s], w_rs.at[dr, s, ch], {"fsdp": to})
+        return remote(src, wbuf.at[q, share, cols], w_ss.at[dr, s], w_rs.at[q - dr, ch], {"fsdp": to})
 
     def w_share(dr, s, ch, q, k):
         region = wbuf.at[q, share, pl.ds(chunks[ch][0], chunks[ch][1])]
-        return remote(region, region, wf_ss.at[dr, s], wf_rs.at[dr, s, ch], {"context": lax.rem(c + k, nc)})
+        return remote(region, region, wf_ss.at[q - dr], wf_rs.at[q - dr, ch], {"context": lax.rem(c + k, nc)})
 
     def has_next(dr):
         return f + 1 < nf if dr == 0 else f >= 1
@@ -188,11 +189,11 @@
     def w_ready(slot, ch):
         region = wbuf.at[order[slot], 0 : (nc - 1) * R, pl.ds(chunks[ch][0], chunks[ch][1])]
         if nc > 1:
-            landed(region, wf_rs.at[way[slot], dist[slot], ch])
+            landed(region, wf_rs.at[order[slot] - way[slot], ch])
 
     def send_gate(e):
         cols = pl.ds(pl.multiple_of(pt[e] * LW, 128), LW)
-        return copy(z_ref.at[:, cols], z_all.at[own_rows, :], z_ss.at[0], z_rs.at[e], {"tensor": pt[e]})
+        return copy(z_ref.at[:, cols], z_all.at[own_rows, :], z_ss.at[0], z_rs.at[e - 1], {"tensor": pt[e]})
 
     early = nt - 1 if nt > 2 else nt
     for e in range(1, early):
@@ -214,7 +215,7 @@
     for j in range(2 * N // 128):
         bc_all[own_rows, j * 128 : (j + 1) * 128] = conv(bc_ref, halo_bc, j * 128, wide0 + j * 128)
     bcs = [
-        copy(bc_all.at[own_rows, :], bc_all.at[own_rows, :], bc_ss.at[0], bc_rs.at[e], {"tensor": pt[e]})
+        copy(bc_all.at[own_rows, :], bc_all.at[own_rows, :], bc_ss.at[0], bc_rs.at[e - 1], {"tensor": pt[e]})
         for e in range(1, nt)
     ]
     xs = []
@@ -234,7 +235,7 @@
             x_send[e - 1, :, lanes] = val
 
         conv_group(e, put)
-        xs.append(copy(x_send.at[e - 1], x_all.at[own_rows, :], x_ss.at[0], x_rs.at[e], {"tensor": pt[e]}))
+        xs.append(copy(x_send.at[e - 1], x_all.at[own_rows, :], x_ss.at[0], x_rs.at[e - 1], {"tensor": pt[e]}))
     def put_own(lanes, val):
         x_all[own_rows, lanes] = val
 
@@ -325,15 +326,13 @@
     msg[0:N, :] = state.astype(BF)
 
     def state_copy(k, src):
-        return remote(msg, st_in.at[src], st_ss.at[k], st_rs.at[k], {"context": lax.rem(c + k, nc)})
+        return remote(msg, st_in.at[src], st_ss.at[k - 1], st_rs.at[k - 1], {"context": lax.rem(c + k, nc)})
 
     for k in range(1, nc):
         @pl.when(c + k < nc)
         def _(k=k):
             state_copy(k, c).start()
 
-    if steps > 1:
-        w_arrive(1, 0)
     for k in range(1, nc):
         @pl.when(c >= k)
         def _(k=k):
@@ -346,7 +345,6 @@
         return carry
 
     lax.fori_loop(0, c, chain, 0)
-    own_w.wait()
     skip = skip_s[0:1, :]
     ones = jnp.ones((8, LW), BF)
 
@@ -377,11 +375,14 @@
             def _(j=j):
                 to_y(u, j, bx, 1).start()
 
+    def near_cols(u):
+        return pl.ds(units[u][1] - chunks[0][1], units[u][2])
+
     def send_unit(u):
-        if u == len(units) - 1:
-            for e in range(1, nt):
+        if u >= nf:
+            for e in range(nt - 1, 0, -1):
                 remote(
-                    rs_send.at[lax.div(pt[e], nx), lax.rem(pt[e], nx), :, spans[u]], rs_near.at[e - 1],
+                    rs_send.at[lax.div(pt[e], nx), lax.rem(pt[e], nx), :, spans[u]], rs_near.at[e - 1, :, near_cols(u)],
                     rs_ss.at[2], rs_rs.at[u, 0], {"tensor": pt[e]},
                 ).start()
             return
@@ -423,6 +424,10 @@
             own_z.wait()
 
         if steps > 1:
+            @pl.when(e == 1)
+            def _():
+                w_arrive(1, 0)
+
             @pl.when(e == nt - 1)
             def _():
                 for ch in range(1, nch - 1):
@@ -431,7 +436,7 @@
         @pl.when(e > 0)
         def _():
             remote(
-                z_ref.at[:, own_cols], z_all.at[rows, :], z_ss.at[0], z_rs.at[e], {"tensor": b}
+                z_ref.at[:, own_cols], z_all.at[rows, :], z_ss.at[0], z_rs.at[e - 1], {"tensor": b}
             ).wait_recv()
 
         start = (stl[b, 0:N, :] + stl[b, N : N + 1, :] * inc_s[...]).astype(BF)
@@ -511,11 +516,11 @@
     landed(gb_in.at[1:nt], ga_rs.at[0])
     def finish(u):
         cols = spans[u]
-        if u == len(units) - 1:
-            landed(rs_near, rs_rs.at[u, 0])
+        if u >= nf:
+            landed(rs_near.at[:, :, near_cols(u)], rs_rs.at[u, 0])
             acc = rs_send[yi, xi, :, cols].astype(F32)
             for e in range(1, nt):
-                acc = acc + rs_near[e - 1].astype(F32)
+                acc = acc + rs_near[e - 1, :, near_cols(u)].astype(F32)
         else:
             landed(sums_in.at[:, :, cols], rs_rs.at[u, 1])
             up_part = rs_send[yi, xi, top, cols].astype(F32) + rs_in[yi, :, cols].astype(F32)
@@ -543,42 +548,66 @@
         return pl.ds(pl.multiple_of(jnp.minimum(i * per, lanes - per) * 128, 128), per * 128)
 
     ccs = [
-        copy(comb.at[:, seg(lax.rem(c + k, nc))], comb_c.at[k], cc_ss.at[k], cc_rs.at[k], {"context": lax.rem(c + k, nc)})
+        copy(comb.at[:, seg(lax.rem(c + k, nc))], comb_c.at[k], cc_ss.at[k - 1], cc_rs.at[k - 1], {"context": lax.rem(c + k, nc)})
         for k in range(1, nc)
     ]
-    last = nf - 1
-    for u in range(2, last):
-        second(u)
-    near = dist[nf - 1] < steps - 1
-
-    def last_slot(ch):
-        project(last + ch)
-        send_unit(last + ch)
-
-    @pl.when(near)
-    def _():
-        for ch in range(nch):
-            last_slot(ch)
-
-    w_arrive(steps - 1, 0)
-
-    @pl.when(jnp.logical_not(near))
-    def _():
-        last_slot(0)
-
-    finish(0)
     for cp in ccs:
         cp.wait()
     acc = comb[:, seg(c)]
     for k in range(1, nc):
         acc = acc + comb_c[k]
     comb2[...] = acc.astype(BF)
-    comb_f[f] = comb2[...]
+    mid = (nf - 1) // 2
+
+    @pl.when(f != mid)
+    def _():
+        copy(comb2, comb_f.at[f], cf_ss.at[0], cf_rs.at[0], {"fsdp": mid})
+
+    last = nf - 1
+    for u in range(2, last):
+        second(u)
+    near = dist[nf - 1] < steps - 1
+
+    def last_slot(ch):
+        project(last + ch)
+        send_unit(last + ch)
+
+    @pl.when(near)
+    def _():
+        for ch in range(nch):
+            last_slot(ch)
+
+    w_arrive(steps - 1, 0)
+
+    @pl.when(jnp.logical_not(near))
+    def _():
+        last_slot(0)
+
+    finish(0)
+    @pl.when(f == mid)
+    def _():
+        landed(comb_f.at[0 : nf - 1], cf_rs.at[0])
+        comb_f[mid] = comb2[...]
+        acc = comb_f[0].astype(F32)
+        for k in range(1, nf):
+            acc = acc + comb_f[k].astype(F32)
+        tot[...] = acc.astype(BF)
+        for k in range(1, nf):
+            copy(tot, tot, tot_ss.at[0], tot_rs.at[0], {"fsdp": lax.rem(mid + k, nf)})
+
     finish(1)
-    for k in range(1, nf):
-        copy(comb2, comb_f.at[f], cf_ss.at[0], cf_rs.at[0], {"fsdp": lax.rem(f + k, nf)})
     for ch in range(1, nch):
         w_arrive(steps - 1, ch)
+        if ch == nch - 1:
+            @pl.when(f != mid)
+            def _():
+                landed(tot, tot_rs.at[0])
+
+            sgs = [
+                copy(tot, seg_in.at[c], sg_ss.at[k - 1], sg_rs.at[k - 1], {"context": lax.rem(c + k, nc)})
+                for k in range(1, nc)
+            ]
+            seg_in[c] = tot[...]
 
         @pl.when(jnp.logical_not(near))
         def _(ch=ch):
@@ -588,22 +617,13 @@
             for u in range(2, last):
                 finish(u)
             second(last)
-    landed(comb_f.at[0 : nf - 1], cf_rs.at[0])
-    acc = comb_f[0].astype(F32)
-    for k in range(1, nf):
-        acc = acc + comb_f[k].astype(F32)
-    seg_own[...] = acc
-    sgs = [copy(seg_own, seg_in.at[c], sg_ss.at[k], sg_rs.at[k], {"context": lax.rem(c + k, nc)}) for k in range(1, nc)]
-    seg_in[c] = acc
-    for ch in range(1, nch - 1):
-        second(last + ch)
     for cp in sgs:
         cp.wait()
     for i in range(nc):
-        full[:, seg(i)] = seg_in[i]
+        full[:, seg(i)] = seg_in[i].astype(F32)
     ga_ref[...] = full[:, 0:LW]
     fin[t] = full[:, LW : LW + part].astype(BF)
-    for e in range(1, nt):
+    for e in range(nt - 1, 0, -1):
         copy(fin.at[t], fin.at[t], fin_ss.at[0], fin_rs.at[0], {"tensor": pt[e]})
     for ch in range(nch):
         finish(last + ch)
@@ -621,9 +641,17 @@
     sent(ad_in.at[1:nt], ad_ss.at[0])
     sent(ag_all.at[0 : nt - 1], ag_ss.at[0])
     sent(gb_in.at[1:nt], ga_ss.at[0])
-    sent(comb_f.at[0 : nf - 1], cf_ss.at[0])
+
+    @pl.when(f != mid)
+    def _():
+        sent(comb2, cf_ss.at[0])
+
+    @pl.when(f == mid)
+    def _():
+        sent(comb_f.at[0 : nf - 1], tot_ss.at[0])
+
     sent(fin.at[0 : nt - 1], fin_ss.at[0])
-    head = slice(0, rs_in.shape[2] - chunks[-1][1])
+    head = slice(0, rs_in.shape[2] - W + chunks[0][1])
     sent(rs_in.at[:, :, head], rs_ss.at[0])
     sent(sums_in.at[:, :, head], rs_ss.at[1])
     sent(rs_near, rs_ss.at[2])
@@ -636,7 +664,7 @@
             if nc > 1:
                 @pl.when(gets(dr, s))
                 def _(dr=dr, s=s):
-                    sent(wbuf.at[0, 0 : (nc - 1) * R, :], wf_ss.at[dr, s])
+                    sent(wbuf.at[0, 0 : (nc - 1) * R, :], wf_ss.at[came(dr, s) - dr])
 
 
 def write_out(mixed, ga, gb, mixed_out, ga_out, gb_out, sem):
@@ -672,7 +700,7 @@
     D = pltpu.SemaphoreType.DMA
     scratch = [
         V((L, full), BF), V((L, BC), BF), V(dt.shape, BF), V(taps.shape, F32), V((full + BC,), F32), V((LW,), F32),
-        V(down.shape, BF), V(up.shape, BF), V((L, M), BF),
+        V(down.shape, BF), V(up.shape, BF), V((L, M), BF), V((1, hl), F32), V((1, hl), F32), V((1, hl), F32),
         V((HALO, full), BF), V((HALO, BC), BF), V((nt - 1, L, LW), BF), V((T, LW), BF), V((T, LW), BF),
         V((T, BC), BF), V((nt,) + dt.shape, BF), V((nf, LW, W), BF), V((T, 128), F32), V((T, 128), F32),
         V((nt, HR, L), F32), V((nt, HR, L), F32),
@@ -680,18 +708,18 @@
         V((128, LW), F32), V((T, LW), F32), V((T, LW), BF), V((nt, 24, L), F32), V((nt, 24, L), F32),
         V((16, L), BF), V((nt, 16, L), BF), V((16, M), BF), V((nt, 16, part), BF),
         V((16, LW + part), F32), V((nc, 16, SW), F32), V((16, SW), BF), V((nf, 16, SW), BF),
-        V((16, SW), F32), V((nc, 16, SW), F32), V((16, LW + part), F32),
+        V((16, SW), BF), V((nc, 16, SW), BF), V((16, LW + part), F32),
         V((nt, 16, part), BF), V((ny, nx, L, M), BF), V((ny + (ny - 1) * nx, L // 2, M), BF),
-        V((ny, L // 2, M), BF), V((ny, L // 2, M), BF), V((nt - 1, L, column_chunks(W)[-1][1]), BF),
-        D((9,)), D((2,)), D((2,)), D((1,)), D((1,)), D((1,)), D((nt,)), D((1,)), D((nt,)), D((1,)), D((nt,)),
-        D((2, nf - 1)), D((2, nf - 1, nch)), D((2, nf - 1)), D((2, nf - 1, nch)), D((nc,)), D((nc,)),
-        D((1,)), D((1,)), D((1,)), D((1,)), D((1,)), D((1,)), D((nc,)), D((nc,)), D((1,)), D((1,)),
-        D((nc,)), D((nc,)), D((1,)), D((1,)), D((3,)), D((units, 2)), D((2,)),
+        V((ny, L // 2, M), BF), V((ny, L // 2, M), BF), V((nt - 1, L, W - column_chunks(W)[0][1]), BF),
+        D((12,)), D((2,)), D((2,)), D((1,)), D((1,)), D((1,)), D((nt - 1,)), D((1,)), D((nt - 1,)), D((1,)), D((nt - 1,)),
+        D((2, nf - 1)), D((nf - 1, nch)), D((nf - 1,)), D((nf - 1, nch)), D((nc - 1,)), D((nc - 1,)),
+        D((1,)), D((1,)), D((1,)), D((1,)), D((1,)), D((1,)), D((nc - 1,)), D((nc - 1,)), D((1,)), D((1,)), D((1,)), D((1,)),
+        D((nc - 1,)), D((nc - 1,)), D((1,)), D((1,)), D((3,)), D((units, 2)), D((2,)),
     ]
     mixed, ga, gb = pl.pallas_call(
         functools.partial(kernel, nt, nf, nc, hl),
         out_shape=(V((L, M), BF), V((16, LW), F32), V((16, M), F32)),
-        in_specs=[hbm, hbm, hbm, hbm, hbm, hbm, vm, vm, vm, hbm, hbm, hbm, hbm, hbm],
+        in_specs=[hbm] * 14,
         out_specs=(vm, vm, vm),
         scratch_shapes=scratch,
         compiler_params=pltpu.CompilerParams(

time: 70.4 us -> 69.3 us (0.984)
  Pallas kernels: 69.6 us -> 68.5 us
    pallas_call x1, Pallas kernels: 68.7 us -> 67.5 us  [shards(): pl.pallas_call(functools.partial(kernel, nt, nf, nc, hl), out_shape=(V((L...]
where the time goes in v6:
time: 69.3 us; the launch traced here: 69.1 us
  Pallas kernels  68.5 us (99%)
    pallas_call x1, Pallas kernels, shards(): pl.pallas_call(functools.partial(kernel, nt, nf, nc, hl), out_shape=(V((L...  67.5 us

profile of v6, /device:TPU:0, one launch (start us, length us, event | category | flops | bytes accessed | tf_op | source)
XLA Modules:
  0.0 69.1 jit_solution(10764356642176361032)
XLA Ops:
  0.6 67.5 %shard_map.157 = (bf16[128,2560]{1,0:T(8,128)(2,1)S(1)}, f32[16,1280]{1,0:T(8,128)S(1)}, f32[16,2560]{1,0:T(8,128)S(1)}) custom-call(bf16[128,5120]{1,0:T(8,128)(2,1)} %bitcast.13, bf16[128,256]{1,0:T(8,128)(2,1)} %bitcast.16, bf16[128,5120]{1,0:T(8,128)(2,1)} %bitcast.14, bf16[80,128]{1,0:T(8,128)(2,1)} %bitcast.18, f32[4,5376]{1,0:T(4,128)} %taps_hbm.1, ...), custom_call_target="tpu_custom_call" | custom-call | tf_op jit(solution)/shard_map/pallas_call | solution.py:719
  68.2 0.9 %shard_map.158 = (bf16[128,2560]{1,0:T(8,128)(2,1)}, f32[16,1280]{1,0:T(8,128)}, f32[16,2560]{1,0:T(8,128)}) custom-call(bf16[128,2560]{1,0:T(8,128)(2,1)S(1)} %get-tuple-element.9.mixed, f32[16,1280]{1,0:T(8,128)S(1)} %get-tuple-element.10.ga, f32[16,2560]{1,0:T(8,128)S(1)} %get-tuple-element.11.gb), custom_call_target="tpu_custom_call" | custom-call | tf_op jit(solution)/shard_map/pallas_call | solution.py:730

commit v7 on v6

--- a/solution.py
+++ b/solution.py
@@ -563,6 +563,7 @@
     def _():
         copy(comb2, comb_f.at[f], cf_ss.at[0], cf_rs.at[0], {"fsdp": mid})
 
+    w_arrive(steps - 1, 0)
     last = nf - 1
     for u in range(2, last):
         second(u)
@@ -577,7 +578,6 @@
         for ch in range(nch):
             last_slot(ch)
 
-    w_arrive(steps - 1, 0)
 
     @pl.when(jnp.logical_not(near))
     def _():
@@ -608,6 +608,14 @@
                 for k in range(1, nc)
             ]
             seg_in[c] = tot[...]
+            for cp in sgs:
+                cp.wait()
+            for i in range(nc):
+                full[:, seg(i)] = seg_in[i].astype(F32)
+            ga_ref[...] = full[:, 0:LW]
+            fin[t] = full[:, LW : LW + part].astype(BF)
+            for e in range(nt - 1, 0, -1):
+                copy(fin.at[t], fin.at[t], fin_ss.at[0], fin_rs.at[0], {"tensor": pt[e]})
 
         @pl.when(jnp.logical_not(near))
         def _(ch=ch):
@@ -617,14 +625,6 @@
             for u in range(2, last):
                 finish(u)
             second(last)
-    for cp in sgs:
-        cp.wait()
-    for i in range(nc):
-        full[:, seg(i)] = seg_in[i].astype(F32)
-    ga_ref[...] = full[:, 0:LW]
-    fin[t] = full[:, LW : LW + part].astype(BF)
-    for e in range(nt - 1, 0, -1):
-        copy(fin.at[t], fin.at[t], fin_ss.at[0], fin_rs.at[0], {"tensor": pt[e]})
     for ch in range(nch):
         finish(last + ch)
     landed(fin.at[0 : nt - 1], fin_rs.at[0])

time: 69.3 us -> 69 us (level)
  no operation moved by 1% of the time
where the time goes in v7:
time: 69 us; the launch traced here: 68.9 us
  Pallas kernels  68.2 us (99%)
    pallas_call x1, Pallas kernels, shards(): pl.pallas_call(functools.partial(kernel, nt, nf, nc, hl), out_shape=(V((L...  67.3 us

profile of v7, /device:TPU:0, one launch (start us, length us, event | category | flops | bytes accessed | tf_op | source)
XLA Modules:
  0.0 68.9 jit_solution(14230570554372698400)
XLA Ops:
  0.6 67.3 %shard_map.157 = (bf16[128,2560]{1,0:T(8,128)(2,1)S(1)}, f32[16,1280]{1,0:T(8,128)S(1)}, f32[16,2560]{1,0:T(8,128)S(1)}) custom-call(bf16[128,5120]{1,0:T(8,128)(2,1)} %bitcast.13, bf16[128,256]{1,0:T(8,128)(2,1)} %bitcast.16, bf16[128,5120]{1,0:T(8,128)(2,1)} %bitcast.14, bf16[80,128]{1,0:T(8,128)(2,1)} %bitcast.18, f32[4,5376]{1,0:T(4,128)} %taps_hbm.1, ...), custom_call_target="tpu_custom_call" | custom-call | tf_op jit(solution)/shard_map/pallas_call | solution.py:719
  68.0 0.9 %shard_map.158 = (bf16[128,2560]{1,0:T(8,128)(2,1)}, f32[16,1280]{1,0:T(8,128)}, f32[16,2560]{1,0:T(8,128)}) custom-call(bf16[128,2560]{1,0:T(8,128)(2,1)S(1)} %get-tuple-element.9.mixed, f32[16,1280]{1,0:T(8,128)S(1)} %get-tuple-element.10.ga, f32[16,2560]{1,0:T(8,128)S(1)} %get-tuple-element.11.gb), custom_call_target="tpu_custom_call" | custom-call | tf_op jit(solution)/shard_map/pallas_call | solution.py:730
